TPU v7x, 256 devices: a whole 4x4x8 slice. The times are simulated.
256 devices in a mesh: grp: 2 (over x_hi), tile: 32 (over x_lo, z, core), mem: 4 (over y).
Axes of the slice: x: 4 (x_hi: 2, x_lo: 2; x = x_hi * 2 + x_lo), y: 4, z: 8, core: 2. Of those that a mesh axis runs over, the one named last changes fastest.
Arguments:
- ens_coarse: bfloat16 [2, 80, 128, 128, 128], P('grp', 'mem', None, 'tile'), may hold values from -6 to 6
- col_interp: bfloat16 [256, 128], replicated, may hold values from -0.5 to 0.5
- row_weights: bfloat16 [3, 256], replicated, may hold values from 0.099609375 to 0.8984375
- ctrl_vec: float32 [2, 128, 256, 256], P('grp', None, 'tile'), may hold values from -24 to 24
- band_loc: bfloat16 [256, 24], P('tile'), may hold values from -1.25 to 1.25
- row_loc: bfloat16 [256, 256], replicated, may hold values from -0.375 to 0.375
- level_loc: bfloat16 [128, 128], replicated, may hold values from -0.5 to 0.5
- hx_pert: bfloat16 [2, 80, 262144], P('grp', None, ('tile', 'mem')), may hold values from -3 to 3
- innov: float32 [2, 262144], P('grp', ('tile', 'mem')), may hold values from -48 to 48
- obs_prec: float32 [2, 262144], P('grp', ('tile', 'mem')), may hold values from 0.3 to 3
- obs_region: int32 [2, 262144], P('grp', ('tile', 'mem')), may hold values from 0 to 7
Outputs:
- increment: float32 [2, 128, 256, 256], P('grp', 'mem', 'tile')
- letkf_weights: float32 [256, 80], P('tile')
Inputs may be any that keep to these rules, and one draw needn't show every extreme that they name: `obs_region`: the region of an observation among the 8 regions of its block of 8192 observations.
All inputs are finite; a program needn't handle non-finite values.
Results may differ from a plain program's by a relative error of at most 0.018.
Values may be sent and summed in bfloat16 or wider, within the bound.
A program may use at most 128 MiB of HBM per device.

v0:
```python
import jax
import jax.numpy as jnp
from jax import lax
from jax.sharding import PartitionSpec as P

NREG = 8


def from_everyone(value, axis):
    copies = jnp.broadcast_to(value, (lax.axis_size(axis), *value.shape))
    return lax.all_to_all(copies, axis, split_axis=0, concat_axis=0, tiled=True)


def over_copies(value, axis):
    everything = from_everyone(value, axis)
    return jnp.sum(everything, axis=0)


def packed_total(arrays, axis):
    ends = [0]
    for a in arrays:
        ends.append(ends[-1] + a.size)
    so_far = over_copies(jnp.concatenate([a.ravel() for a in arrays]), axis)
    return tuple((so_far[b:e].reshape(a.shape) for a, b, e in zip(arrays, ends, ends[1:])))


def extended(value, sides, width):
    for axis, dim in sides:
        peers, length = (lax.axis_size(axis), value.shape[dim])
        up = [(i, (i + 1) % peers) for i in range(peers - 1)]
        down = [(j, i) for i, j in up]
        last = lax.slice_in_dim(value, length - width, length, axis=dim)
        first = lax.slice_in_dim(value, 0, width, axis=dim)
        before = lax.ppermute(last, axis, up)
        after = lax.ppermute(first, axis, down)
        value = jnp.concatenate([before, value, after], axis=dim)
    return value


def split_up(value, dim, peers):
    before, after = (value.shape[:dim], value.shape[dim + 1 :])
    return jnp.moveaxis(value.reshape(*before, peers, -1, *after), dim, 0)


def summed_on_arrival(value, axis, dim):
    blocks = split_up(value, dim, lax.axis_size(axis))
    arrived = lax.all_to_all(blocks, axis, split_axis=0, concat_axis=0, tiled=True)
    return arrived.astype(jnp.float32).sum(axis=0)


def row_matrix(row_weights, fine_rows, coarse_rows):
    fine_index = lax.broadcasted_iota(jnp.int32, (fine_rows, coarse_rows), 0)
    coarse_index = lax.broadcasted_iota(jnp.int32, (fine_rows, coarse_rows), 1)
    weights = row_weights.astype(jnp.float32)
    stencil = jnp.zeros((fine_rows, coarse_rows), jnp.float32)
    for offset in range(3):
        matched = coarse_index == fine_index // 2 + offset - 1
        stencil = stencil + jnp.where(matched, weights[offset][:, None], 0.0)
    return stencil.astype(jnp.bfloat16)


def solve_weights(gram_sums, right_side):
    member_count = gram_sums.shape[-1]
    system = gram_sums + (member_count - 1) * jnp.eye(member_count, dtype=jnp.float32)
    factor = jnp.linalg.cholesky(system)
    halfway = lax.linalg.triangular_solve(factor, right_side[..., None], left_side=True, lower=True)
    result = lax.linalg.triangular_solve(
        factor, halfway, left_side=True, lower=True, transpose_a=True
    )
    return result[..., 0]


def body(
    ens_coarse,
    col_interp,
    row_weights,
    ctrl_vec,
    band_loc,
    row_loc,
    level_loc,
    hx_pert,
    innov,
    obs_prec,
    obs_region,
):
    fine_rows = row_weights.shape[1]
    columns = band_loc.shape[0]
    total_members = hx_pert.shape[1]
    observed = hx_pert[0]
    weighted = (observed * obs_prec[0][None, :]).astype(jnp.bfloat16)
    labels = lax.broadcasted_iota(jnp.int32, (NREG, observed.shape[1]), 0)
    member_of = obs_region[0][None, :] == labels
    masked = jnp.where(member_of[:, None, :], weighted[None], jnp.zeros((), jnp.bfloat16))
    gram_sums = jnp.einsum("rko,jo->rkj", masked, observed, preferred_element_type=jnp.float32)
    innov_rows = jnp.where(member_of, innov[0][None, :], 0.0)
    right_side = jnp.dot(innov_rows, weighted.astype(jnp.float32).T)
    gram_sums, right_side = packed_total((gram_sums, right_side), ("grp", "mem"))
    coarse_cols = jnp.einsum(
        "tklic,jc->tklij", ens_coarse, col_interp, preferred_element_type=jnp.float32
    ).astype(jnp.bfloat16)
    stencil = row_matrix(row_weights, fine_rows, fine_rows // 2)
    refined = jnp.einsum(
        "tklij,ri->tkljr",
        lax.all_to_all(coarse_cols, "tile", split_axis=4, concat_axis=3, tiled=True),
        stencil,
        preferred_element_type=jnp.float32,
    ).astype(jnp.bfloat16)
    member_fine = refined[0]
    slot_term = member_fine * ctrl_vec[0][None]
    projected = summed_on_arrival(slot_term.astype(jnp.bfloat16), "grp", 0).astype(jnp.bfloat16)
    padded = extended(projected, (("tile", 2),), columns)
    banded = jnp.einsum(
        "jq,klqr->kljr", band_loc, padded, preferred_element_type=jnp.float32
    ).astype(jnp.bfloat16)
    row_mixed = jnp.einsum(
        "kljs,rs->kljr", banded, row_loc, preferred_element_type=jnp.float32
    ).astype(jnp.bfloat16)
    localized = lax.all_gather(
        jnp.einsum(
            "lm,kmjr->kljr", level_loc, row_mixed, preferred_element_type=jnp.float32
        ).astype(jnp.bfloat16),
        "grp",
        axis=0,
        tiled=True,
    )
    increment = lax.psum_scatter(
        jnp.sum(member_fine.astype(jnp.float32) * localized.astype(jnp.float32), axis=0),
        "mem",
        scatter_dimension=0,
        tiled=True,
    ) / (total_members - 1)
    per_device = NREG // lax.axis_size("mem")
    first_region = lax.axis_index("mem") * per_device
    own_weights = solve_weights(
        lax.dynamic_slice_in_dim(gram_sums, first_region, per_device, 0),
        lax.dynamic_slice_in_dim(right_side, first_region, per_device, 0),
    )
    weights = lax.all_gather(own_weights, "mem", axis=0, tiled=True)
    return (increment[None], weights)


def solution(mesh):
    placed = (
        P("grp", "mem", None, "tile", None),
        P(),
        P(),
        P("grp", None, "tile", None),
        P("tile", None),
        P(),
        P(),
        P("grp", None, ("tile", "mem")),
        P("grp", ("tile", "mem")),
        P("grp", ("tile", "mem")),
        P("grp", ("tile", "mem")),
    )
    return jax.shard_map(
        body,
        mesh=mesh,
        in_specs=placed,
        out_specs=(P("grp", "mem", "tile", None), P("tile", None)),
        check_vma=False,
    )
```

profile of v0, /device:TPU:2, one launch (start us, length us, event | category | flops | bytes accessed | tf_op | source)
XLA Modules:
  0.0 598.9 jit_solution(5206151836381627881)
XLA Ops:
  7.2 5.6 convert_bitcast_fusion.1
  12.8 9.7 %copy.61 = bf16[1,20,128,4,256]{2,3,1,0,4:T(4,128)(2,1)} copy(bf16[1,20,128,4,256]{4,2,3,1,0:T(8,128)(2,1)} %convert_bitcast_fusion.1) | data formatting | bytes 10485760 | tf_op jit(solution)/shard_map/convert_element_type | solution.py:100
  22.5 10.3 %all-to-all-start = ((bf16[1,20,128,4,256]{2,3,1,0,4:T(4,128)(2,1)}), bf16[1,20,128,4,256]{2,3,1,0,4:T(4,128)(2,1)}, u32[]{:S(2)}, u32[]{:S(2)}) async-start(bf16[1,20,128,4,256]{2,3,1,0,4:T(4,128)(2,1)} %copy.61), calls=%async_computation | async-start | bytes 10485760 | tf_op jit(solution)/shard_map/all_to_all | solution.py:104
  33.2 116.2 %all-to-all-done = bf16[1,20,128,4,256]{2,3,1,0,4:T(4,128)(2,1)} async-done(((bf16[1,20,128,4,256]{2,3,1,0,4:T(4,128)(2,1)}), bf16[1,20,128,4,256]{2,3,1,0,4:T(4,128)(2,1)}, u32[]{:S(2)}, u32[]{:S(2)}) %all-to-all-start) | async-done | bytes 5242912 | tf_op jit(solution)/shard_map/all_to_all | solution.py:104
  149.4 3.8 copy.100
  153.3 3.3 copy.63
  156.6 5.6 convert_convert_fusion
  162.2 2.9 multiply_convert_fusion
  165.1 4.0 copy-done.1
  169.2 120.8 %all_to_all.26 = bf16[2,10,128,8,256]{4,2,3,1,0:T(8,128)(2,1)} all-to-all(bf16[2,10,128,8,256]{4,2,3,1,0:T(8,128)(2,1)S(1)} %multiply_convert_fusion), channel_id=1, replica_groups=mesh['grp'=2,'tile'=32,'mem'=4] {'grp'}, dimensions={0} | all-to-all | bytes 20971520 | tf_op jit(solution)/shard_map/all_to_all | solution.py:47
  289.9 10.1 %reduce_sum.30 = bf16[10,128,8,256]{3,1,2,0:T(8,128)(2,1)} reduce(bf16[2,10,128,8,256]{4,2,3,1,0:T(8,128)(2,1)} %all_to_all.26, bf16[]{:T(256)} %constant.85.clone.1), dimensions={0}, to_apply=%region_0.1 | reduce | flops 2621440 | bytes 15728642 | tf_op jit(solution)/shard_map/reduce_sum | solution.py:48
  300.1 5.8 copy.66
  305.9 3.3 collective-permute-start.1
  309.2 2.1 collective-permute-start
  311.3 55.1 %collective-permute-done.1 = bf16[10,128,8,256]{3,2,1,0:T(8,128)(2,1)S(1)} collective-permute-done((bf16[10,128,8,256]{3,2,1,0:T(8,128)(2,1)S(1)}, bf16[10,128,8,256]{3,2,1,0:T(8,128)(2,1)S(1)}, u32[]{:S(2)}, u32[]{:S(2)}) %collective-permute-start.1) | collective-permute-done | bytes 5242912 | tf_op jit(solution)/shard_map/ppermute | solution.py:35
  366.5 2.4 copy-done.9
  368.8 3.7 collective-permute-done
  372.6 9.2 %fusion.18 = bf16[10,128,8,256]{3,2,1,0:T(8,128)(2,1)} fusion(bf16[10,128,8,256]{3,2,1,0:T(8,128)(2,1)} %copy-done.9, bf16[10,128,8,256]{3,2,1,0:T(8,128)(2,1)} %copy-done.2, bf16[10,128,8,256]{3,2,1,0:T(8,128)(2,1)} %collective-permute-done, bf16[256,256]{1,0:T(8,128)(2,1)S(1)} %copy-done, bf16[8,24]{1,0:T(8,128)(2,1)S(1)} %copy-done.11), kind=kOutput, calls=%fused_computation.18 | convolution fusion | flops 1520435200 | bytes 21102976 | tf_op jit(solution)/shard_map/kljs,rs->kljr/dot_general | solution.py:115
  381.8 7.0 %convert_bitcast_fusion = bf16[10,128,8,256]{1,3,2,0:T(8,128)(2,1)} fusion(bf16[10,128,8,256]{3,2,1,0:T(8,128)(2,1)} %fusion.18, bf16[128,128]{1,0:T(8,128)(2,1)S(1)} %copy-done.5), kind=kOutput, calls=%fused_computation.15 | convolution fusion | flops 673710080 | bytes 10518528 | tf_op jit(solution)/shard_map/lm,kmjr->kljr/dot_general | solution.py:119
  388.7 8.7 %copy.70 = bf16[10,128,8,256]{3,2,1,0:T(8,128)(2,1)} copy(bf16[10,128,8,256]{1,3,2,0:T(8,128)(2,1)} %convert_bitcast_fusion) | data formatting | bytes 10485760 | tf_op jit(solution)/shard_map/convert_element_type | solution.py:121
  397.4 0.9 copy-done.4
  398.7 0.8 fusion.24
  399.9 2.1 broadcast_in_dim.95
  401.9 4.5 all-to-all-start.2
  406.7 130.7 %all-gather.3.cloned.1.call-done = bf16[20,128,8,256]{3,2,1,0:T(8,128)(2,1)} async-done(((bf16[10,128,8,256]{3,2,1,0:T(8,128)(2,1)}), bf16[20,128,8,256]{3,2,1,0:T(8,128)(2,1)}) %all-gather.3.cloned.1.call-update) | async-done | bytes 10485776 | tf_op jit(solution)/shard_map/all_gather | solution.py:118
  537.4 13.1 %multiply_reduce_fusion = f32[128,8,256]{2,0,1:T(8,128)} fusion(f32[20,128,8,256]{3,1,2,0:T(8,128)} %copy-done.1, bf16[20,128,8,256]{3,2,1,0:T(8,128)(2,1)} %all-gather.3.cloned.1.call-done), kind=kLoop, calls=%fused_computation | loop fusion | flops 15466496 | bytes 32505856 | tf_op jit(solution)/shard_map/reduce_sum | solution.py:127
  550.7 1.2 reduce_sum.32
  552.5 14.7 %custom-call.9 = f32[2,80,80]{2,1,0:T(8,128)S(1)} custom-call(f32[2,80,80]{2,1,0:T(8,128)S(1)} %fusion.40), custom_call_target="Cholesky" | custom-call | tf_op jit(solution)/shard_map/jit(cholesky)/cholesky | solution.py:65
  567.4 12.3 %custom-call.10 = f32[2,1,80,80]{2,3,1,0:T(8,128)S(1)} custom-call(f32[2,1,80,80]{3,2,1,0:T(8,128)S(1)} %select_bitcast_fusion), custom_call_target="InvertDiagBlocksLowerTriangular" | custom-call | tf_op jit(solution)/shard_map/triangular_solve | solution.py:67
  580.1 9.5 %all-gather = f32[4,2,80]{2,1,0:T(2,128)S(1)} all-gather(f32[1,2,80]{2,1,0:T(2,128)S(1)} %bitcast.98), channel_id=1, replica_groups=mesh['grp'=2,'tile'=32,'mem'=4] {'mem'}, dimensions={0}, use_global_device_ids=true | all-gather | bytes 3200 | tf_op jit(solution)/shard_map/all_gather | solution.py:138
  589.6 1.0 multiply_bitcast_fusion
  590.6 0.9 copy.76
  (57 shorter events, 3.2 us)
Async XLA Ops:
  7.2 365.4 %copy-start = (bf16[256,256]{1,0:T(8,128)(2,1)S(1)}, bf16[256,256]{1,0:T(8,128)(2,1)}, u32[]{:S(2)}) copy-start(bf16[256,256]{1,0:T(8,128)(2,1)} %param.16) | copy-start | bytes 393220
  22.5 10.3 %copy-start.3 = (f32[1,128,8,256]{3,2,1,0:T(8,128)S(1)}, f32[1,128,8,256]{3,2,1,0:T(8,128)}, u32[]{:S(2)}) copy-start(f32[1,128,8,256]{3,2,1,0:T(8,128)} %param.14) | copy-start | bytes 3145732
  22.5 10.7 %copy-start.8 = (bf16[3,256]{1,0:T(4,128)(2,1)S(1)}, bf16[3,256]{1,0:T(4,128)(2,1)}, u32[]{:S(2)}) copy-start(bf16[3,256]{1,0:T(4,128)(2,1)} %param.13) | copy-start | bytes 4612
  22.5 126.9 %all-to-all-start = ((bf16[1,20,128,4,256]{2,3,1,0,4:T(4,128)(2,1)}), bf16[1,20,128,4,256]{2,3,1,0,4:T(4,128)(2,1)}, u32[]{:S(2)}, u32[]{:S(2)}) async-start(bf16[1,20,128,4,256]{2,3,1,0,4:T(4,128)(2,1)} %copy.61), calls=%async_computation | async-start | bytes 10485760 | tf_op jit(solution)/shard_map/all_to_all | solution.py:104
  32.8 504.6 %all-gather.3.cloned.1.call-start = ((), (), s32[]{:S(2)}) async-start(), calls=%async_computation.4 | async-start | bytes 15728640 | tf_op jit(solution)/shard_map/all_gather | solution.py:118
  162.2 7.0 %copy-start.1 = (f32[20,128,8,256]{3,1,2,0:T(8,128)}, f32[20,128,8,256]{3,1,2,0:T(8,128)S(1)}, u32[]{:S(2)}) copy-start(f32[20,128,8,256]{3,1,2,0:T(8,128)S(1)} %convert_convert_fusion) | copy-start | bytes 62914564
  300.1 72.5 %copy-start.11 = (bf16[8,24]{1,0:T(8,128)(2,1)S(1)}, bf16[8,24]{1,0:T(8,128)(2,1)}, u32[]{:S(2)}) copy-start(bf16[8,24]{1,0:T(8,128)(2,1)} %param.15) | copy-start | bytes 1156
  305.9 3.3 copy-start.2
  305.9 75.9 %copy-start.5 = (bf16[128,128]{1,0:T(8,128)(2,1)S(1)}, bf16[128,128]{1,0:T(8,128)(2,1)}, u32[]{:S(2)}) copy-start(bf16[128,128]{1,0:T(8,128)(2,1)} %param.17) | copy-start | bytes 98308
  305.9 60.5 %collective-permute-start.1 = (bf16[10,128,8,256]{3,2,1,0:T(8,128)(2,1)S(1)}, bf16[10,128,8,256]{3,2,1,0:T(8,128)(2,1)S(1)}, u32[]{:S(2)}, u32[]{:S(2)}) collective-permute-start(bf16[10,128,8,256]{3,2,1,0:T(8,128)(2,1)S(1)} %copy.66), channel_id=1, source_target_pairs={{4,0},{8,4},{12,8},{16,12},{20,16},{24,20},{28,24},{32,28},{36,32}... | collective-permute-start | bytes 15728648 | tf_op jit(solution)/shard_map/ppermute | solution.py:35
  309.2 63.4 %collective-permute-start = (bf16[10,128,8,256]{3,2,1,0:T(8,128)(2,1)S(1)}, bf16[10,128,8,256]{3,2,1,0:T(8,128)(2,1)}, u32[]{:S(2)}, u32[]{:S(2)}) collective-permute-start(bf16[10,128,8,256]{3,2,1,0:T(8,128)(2,1)S(1)} %copy.66), channel_id=1, source_target_pairs={{0,4},{4,8},{8,12},{12,16},{16,20},{20,24},{24,28},{28,32},{32,36}... | collective-permute-start | bytes 15728648 | tf_op jit(solution)/shard_map/ppermute | solution.py:34
  366.5 2.4 copy-start.9
  397.4 1.0 copy-start.4
  397.4 1.0 copy-start.6
  397.4 1.0 copy-start.7
  397.4 1.0 copy-start.10
  401.9 148.8 %all-to-all-start.2 = ((f32[8,1,51840]{2,1,0:T(1,128)}), f32[8,1,51840]{2,1,0:T(1,128)S(1)}, u32[]{:S(2)}, u32[]{:S(2)}) async-start(f32[8,1,51840]{2,1,0:T(1,128)} %broadcast_in_dim.95), calls=%async_computation.3 | async-start | bytes 3317760 | tf_op jit(solution)/shard_map/all_to_all | solution.py:11
  406.4 183.2 %reduce-scatter.2.cloned.1.call-start = ((), (), s32[]{:S(2)}) async-start(), calls=%async_computation.5 | async-start | bytes 1310720 | tf_op jit(solution)/shard_map/reduce_scatter | solution.py:126
Sparse Core Ops, SparseCore 0:
  397.5 139.8 all-gather.2
  550.7 26.6 reduce-scatter.1
where the time goes:
time: 602 us; the launch traced here: 599 us
  waiting for transfers between devices  306 us (51%)
  blocking collectives  130 us (22%)
  other arithmetic  55.8 us (9%)
  local copies, waits for them, and re-layouts  43.4 us (7%)
  matrix products  28.8 us (5%)
  starting transfers between devices  20.5 us (3%)
  between operations  14.4 us (2%)
    all_gather x1, waiting for transfers between devices, body(): lax.all_gather(jnp.einsum('lm,kmjr->kljr', level_loc, row_mixed, preferre...  131 us
    all_to_all x1, blocking collectives, summed_on_arrival(): lax.all_to_all(blocks, axis, split_axis=0, concat_axis=0, tiled=True)  121 us
    all_to_all x1, waiting for transfers between devices, body(): lax.all_to_all(coarse_cols, 'tile', split_axis=4, concat_axis=3, tiled=True)  116 us
    ppermute x1, waiting for transfers between devices, extended(): after = lax.ppermute(first, axis, down)  55.1 us
    another operation x4, other arithmetic, solve_weights(): factor = jnp.linalg.cholesky(system)  14.8 us
    reduce_sum x1, other arithmetic, body(): jnp.sum(member_fine.astype(jnp.float32) * localized.astype(jnp.float32),...  13.1 us
    another operation x3, other arithmetic, solve_weights(): lax.linalg.triangular_solve(factor, halfway, left_side=True, lower=True,...  12.4 us
  transfers between devices with their start and end apart: 6, of which 4 were waited for; matrix products, arithmetic and copies ran while one was open for 8% of the time, Pallas kernels for 0%

commit v1 on v0

v1 whole, which is shorter than its diff:
```python
import functools

import jax
import jax.numpy as jnp
from jax import lax
from jax.experimental import pallas as pl
from jax.experimental.pallas import tpu as pltpu
from jax.sharding import Mesh, PartitionSpec as P

NREG = 8
BF = jnp.bfloat16
F32 = jnp.float32
GR = 16
WIN = 10


def spread_kernel(x_ref, ci_ref, o_ref):
    nb, rows, cols, lev = o_ref.shape[1], o_ref.shape[4], o_ref.shape[5], o_ref.shape[6]
    for i in range(rows):
        fine = lax.dot_general(
            ci_ref[...], x_ref[0, i], (((1,), (1,)), ((), ())), preferred_element_type=F32
        )
        o_ref[0, :, 0, 0, i] = fine.astype(BF).reshape(nb, cols, lev)


def window_start(group, coarse_rows):
    return min(max(group * GR // 2 - 1, 0), coarse_rows - WIN)


def refine_group(c_ref, s_ref, t, group, coarse):
    start = window_start(group, coarse)
    cols, lev = c_ref.shape[-2], c_ref.shape[-1]
    window = c_ref[t, pl.ds(start, WIN)].reshape(WIN * cols, lev)
    return jnp.dot(s_ref[group], window, preferred_element_type=F32)


def project_kernel(c_ref, s_ref, ctrl_ref, lo_ref, hi_ref):
    coarse, cols, lev = c_ref.shape[1:]
    half = cols // 2
    for group in range(s_ref.shape[0]):
        rows = pl.ds(group * GR, GR)
        total = None
        for t in range(2):
            fine = refine_group(c_ref, s_ref, t, group, coarse).astype(BF)
            term = fine.astype(F32).reshape(cols, GR, lev) * ctrl_ref[t, :, rows, :].astype(F32)
            total = term if total is None else total + term
        total = total.astype(BF)
        lo_ref[0, :, rows, :] = total[:half]
        hi_ref[0, :, rows, :] = total[half:]


def localize_kernel(
    c_ref, s_ref, lo_ref, hi_ref, left_ref, right_ref, band_ref, row_ref, lev_ref, o_ref, fine, banded, acc
):
    coarse, cols, lev = c_ref.shape[1:]
    k = pl.program_id(0)
    half = cols // 2

    for group in range(s_ref.shape[0]):
        rows = pl.ds(group * GR, GR)
        for t in range(2):
            fine[t, :, rows, :] = (
                refine_group(c_ref, s_ref, t, group, coarse).astype(BF).reshape(cols, GR, lev)
            )
        parts = [ref[0, :, rows, :].reshape(half * GR, lev) for ref in (left_ref, lo_ref, hi_ref, right_ref)]
        stacked = jnp.concatenate(parts, axis=0)
        mixed = jnp.dot(band_ref[...], stacked, preferred_element_type=F32)
        banded[:, rows, :] = mixed.astype(BF).reshape(cols, GR, lev)

    def column(j, carry):
        mixed = jnp.dot(row_ref[...], banded[j], preferred_element_type=F32).astype(BF)
        local = jnp.dot(mixed, lev_ref[...], preferred_element_type=F32)
        for t in range(2):
            term = fine[t, j].astype(F32) * local
            acc[t, j] = jnp.where(k == 0, term, acc[t, j] + term)
        return carry

    lax.fori_loop(0, cols, column, 0)

    @pl.when(k == pl.num_programs(0) - 1)
    def _():
        nl, cn, jn, ll = o_ref.shape[1:5]

        def flip(j, carry):
            for t in range(2):
                turned = acc[t, j].T
                for q in range(nl):
                    o_ref[t, q, j // jn, j % jn] = turned[q * ll : (q + 1) * ll].astype(o_ref.dtype)
            return carry

        lax.fori_loop(0, cols, flip, 0)


def row_stencils(row_weights, coarse_rows, cols):
    fine_rows = row_weights.shape[1]
    groups = fine_rows // GR
    weights = row_weights.reshape(3, groups, GR)
    starts = jnp.array([window_start(g, coarse_rows) for g in range(groups)])
    fine_row = jnp.arange(fine_rows).reshape(groups, GR)
    coarse_row = starts[:, None] + jnp.arange(WIN)[None, :]
    total = jnp.zeros((groups, GR, WIN), BF)
    for s in range(3):
        hit = coarse_row[:, None, :] == (fine_row // 2 + s - 1)[:, :, None]
        total = total + jnp.where(hit, weights[s][:, :, None], jnp.zeros((), BF))
    eye = jnp.eye(cols, dtype=BF)
    full = eye[None, :, None, None, :] * total[:, None, :, :, None]
    return full.reshape(groups, cols * GR, WIN * cols)


def band_matrix(band):
    cols, width = band.shape
    step = width // 3
    pieces = []
    for b in range(cols // step):
        rows = band[b * step : (b + 1) * step]
        pieces.append(jnp.pad(rows, ((0, 0), (b * step, cols - step - b * step))))
    full = jnp.concatenate(pieces, axis=0)
    eye = jnp.eye(GR, dtype=BF)
    big = full[:, None, :, None] * eye[None, :, None, :]
    return big.reshape(cols * GR, full.shape[1] * GR)


def solve_weights(gram_sums, right_side):
    member_count = gram_sums.shape[-1]
    system = gram_sums + (member_count - 1) * jnp.eye(member_count, dtype=F32)
    factor = jnp.linalg.cholesky(system)
    halfway = lax.linalg.triangular_solve(factor, right_side[..., None], left_side=True, lower=True)
    result = lax.linalg.triangular_solve(
        factor, halfway, left_side=True, lower=True, transpose_a=True
    )
    return result[..., 0]


def letkf(hx_pert, innov, obs_prec, obs_region):
    observed = hx_pert[0]
    members = observed.shape[0]
    weighted = (observed * obs_prec[0][None, :]).astype(BF)
    labels = lax.broadcasted_iota(jnp.int32, (NREG, observed.shape[1]), 0)
    member_of = obs_region[0][None, :] == labels
    masked = jnp.where(member_of[:, None, :], weighted[None], jnp.zeros((), BF))
    gram = jnp.einsum("rko,jo->rkj", masked, observed, preferred_element_type=F32)
    innov_rows = jnp.where(member_of, innov[0][None, :], 0.0)
    right = jnp.dot(innov_rows, weighted.astype(F32).T)
    packed = jnp.concatenate([gram.reshape(NREG, -1), right], axis=1)
    arrived = lax.all_to_all(packed[:, None], ("xh", "y"), split_axis=0, concat_axis=0, tiled=True)
    total = jnp.sum(arrived, axis=0)
    size = members * members
    own = solve_weights(total[:, :size].reshape(-1, members, members), total[:, size:])
    return lax.all_gather(own, ("xh", "y"), axis=0, tiled=True)


def body(
    ens_coarse,
    col_interp,
    row_weights,
    ctrl_vec,
    band_loc,
    row_loc,
    level_loc,
    hx_pert,
    innov,
    obs_prec,
    obs_region,
):
    nxh, nxl, nz, nc, ny = (lax.axis_size(a) for a in ("xh", "xl", "z", "c", "y"))
    _, members, lev, own_rows, coarse_cols = ens_coarse.shape
    fine_cols = col_interp.shape[0]
    fine_rows = row_weights.shape[1]
    blocks = nxl * nz
    cols = fine_cols // blocks
    group = members // (nxh * nc)
    tiles = nxl * nz * nc
    coarse = tiles * own_rows
    total_members = hx_pert.shape[1]

    by_row = jnp.transpose(ens_coarse[0], (0, 2, 1, 3))
    spread = pl.pallas_call(
        spread_kernel,
        grid=(members,),
        in_specs=[
            pl.BlockSpec((1, own_rows, lev, coarse_cols), lambda k: (k, 0, 0, 0)),
            pl.BlockSpec((fine_cols, coarse_cols), lambda k: (0, 0)),
        ],
        out_specs=pl.BlockSpec(
            (1, blocks, 1, 1, own_rows, cols, lev),
            lambda k: (k // (nc * group), 0, (k // group) % nc, k % group, 0, 0, 0),
        ),
        out_shape=jax.ShapeDtypeStruct((nxh, blocks, nc, group, own_rows, cols, lev), BF),
        compiler_params=pltpu.CompilerParams(dimension_semantics=("arbitrary",)),
        cost_estimate=pl.CostEstimate(flops=2 * members * own_rows * lev * coarse_cols * fine_cols, bytes_accessed=8000000, transcendentals=0),
    )(by_row, col_interp)
    spread = spread.reshape(nxh * tiles, group, own_rows, cols, lev)
    arrived = lax.all_to_all(spread, ("xh", "xl", "z", "c"), split_axis=0, concat_axis=0, tiled=True)
    arrived = arrived.reshape(nxh, tiles, group, own_rows, cols, lev)

    turned = jnp.transpose(ctrl_vec[0].astype(BF), (1, 2, 0))
    ctrl = lax.all_gather(turned, ("xh", "c"), axis=0)
    ctrl = ctrl.reshape(nxh, cols, fine_rows, lev)
    band = lax.all_gather(band_loc, "c", axis=0, tiled=True)

    stencils = row_stencils(row_weights, coarse, cols)
    band_full = band_matrix(band)
    lev_t = level_loc.T

    half = cols // 2
    field = jax.ShapeDtypeStruct((group, half, fine_rows, lev), BF)
    field_spec = pl.BlockSpec((1, half, fine_rows, lev), lambda k: (k, 0, 0, 0))
    c_spec = pl.BlockSpec((nxh, tiles, 1, own_rows, cols, lev), lambda k: (0, 0, k, 0, 0, 0))
    params = pltpu.CompilerParams(dimension_semantics=("arbitrary",), vmem_limit_bytes=56 << 20)

    def whole(a):
        return pl.BlockSpec(a.shape, lambda k, n=a.ndim: (0,) * n)

    def flat(c_ref):
        return c_ref.reshape(nxh, coarse, cols, lev)

    def project(c_ref, *rest):
        project_kernel(flat(c_ref), *rest)

    def localize(c_ref, *rest):
        localize_kernel(flat(c_ref), *rest)

    lo, hi = pl.pallas_call(
        project,
        grid=(group,),
        in_specs=[c_spec, whole(stencils), whole(ctrl)],
        out_specs=[field_spec, field_spec],
        out_shape=[field, field],
        compiler_params=params,
    )(arrived, stencils, ctrl)

    up = [(i, i + 1) for i in range(blocks - 1)]
    down = [(i + 1, i) for i in range(blocks - 1)]
    left = lax.ppermute(hi, ("xl", "z"), up)
    right = lax.ppermute(lo, ("xl", "z"), down)

    partial = pl.pallas_call(
        localize,
        grid=(group,),
        in_specs=[c_spec, whole(stencils)]
        + [field_spec] * 4
        + [whole(band_full), whole(row_loc), whole(lev_t)],
        out_specs=pl.BlockSpec(
            (nxh, ny, nc, cols // nc, lev // ny, fine_rows), lambda k: (0, 0, 0, 0, 0, 0)
        ),
        out_shape=jax.ShapeDtypeStruct((nxh, ny, nc, cols // nc, lev // ny, fine_rows), BF),
        scratch_shapes=[
            pltpu.VMEM((nxh, cols, fine_rows, lev), BF),
            pltpu.VMEM((cols, fine_rows, lev), BF),
            pltpu.VMEM((nxh, cols, fine_rows, lev), F32),
        ],
        compiler_params=params,
    )(arrived, stencils, lo, hi, left, right, band_full, row_loc, lev_t)
    partial = partial.reshape(nxh * ny * nc, cols // nc, lev // ny, fine_rows)
    pieces = lax.all_to_all(partial, ("xh", "y", "c"), split_axis=0, concat_axis=0, tiled=True)
    increment = jnp.sum(pieces.astype(F32), axis=0) / (total_members - 1)
    increment = jnp.transpose(increment, (1, 0, 2))

    weights = letkf(hx_pert, innov, obs_prec, obs_region)
    return (increment[None], weights)


def solution(mesh):
    shape = (2, 2, mesh.shape["tile"] // 4, 2, mesh.shape["mem"])
    fine_mesh = Mesh(mesh.devices.reshape(shape), ("xh", "xl", "z", "c", "y"))
    tile = ("xl", "z", "c")
    obs = (*tile, "y")
    placed = (
        P("xh", "y", None, tile, None),
        P(),
        P(),
        P("xh", None, tile, None),
        P(tile, None),
        P(),
        P(),
        P("xh", None, obs),
        P("xh", obs),
        P("xh", obs),
        P("xh", obs),
    )
    return jax.shard_map(
        body,
        mesh=fine_mesh,
        in_specs=placed,
        out_specs=(P("xh", "y", tile, None), P(tile, None)),
        check_vma=False,
    )
```

time: 602 us -> 332 us (0.55)
  waiting for transfers between devices: 306 us -> 131 us
  blocking collectives: 130 us -> 27.8 us
  Pallas kernels: 0 us -> 67.8 us
  other arithmetic: 55.8 us -> 18.4 us
  matrix products: 28.8 us -> 1.33 us
  starting transfers between devices: 20.5 us -> 30.6 us
    all_to_all x1 -> x0, blocking collectives: 121 us -> none  [summed_on_arrival(): lax.all_to_all(blocks, axis, split_axis=0, concat_axis=0, tiled=True)]
    all_gather x1, waiting for transfers between devices: 131 us -> 19.3 us  [body(): ctrl = lax.all_gather(turned, ('xh', 'c'), axis=0)]
    pallas_call x0 -> x3, Pallas kernels: none -> 67.8 us  [the longest x1 43.3 us: body(): pl.pallas_call(localize, grid=(group,), in_specs=[c_spec, whole(stencils)...]
    all_to_all x2 -> x3, waiting for transfers between devices: 116 us -> 69.6 us  [the longest x1 69.6 us: body(): lax.all_to_all(spread, ('xh', 'xl', 'z', 'c'), split_axis=0, concat_axis=...]
    dot_general x6 -> x2, matrix products: 28.4 us -> 1.02 us  [the longest x1 0.83 us: letkf(): jnp.einsum('rko,jo->rkj', masked, observed, preferred_element_type=F32)]
    unnamed x0 -> x1, blocking collectives: none -> 24.7 us
    mul x2 -> x7, local copies, waits for them, and re-layouts: 0.42 us -> 24.8 us  [the longest x6 20.6 us: row_stencils(): full = eye[None, :, None, None, :] * total[:, None, :, :, None]]
    reduce_sum x3 -> x2, other arithmetic: 24.5 us -> 0.55 us  [the longest x1 0.39 us: body(): increment = jnp.sum(pieces.astype(F32), axis=0) / (total_members - 1)]
  transfers between devices with their start and end apart: 6 -> 6, of which waited for: 4 -> 4; matrix products, arithmetic and copies ran while one was open for 8% -> 16% of each run, Pallas kernels for 0% -> 13%
where the time goes in v1:
time: 332 us; the launch traced here: 330 us
  waiting for transfers between devices  131 us (39%)
  Pallas kernels  67.8 us (20%)
  local copies, waits for them, and re-layouts  38 us (11%)
  starting transfers between devices  30.6 us (9%)
  blocking collectives  27.8 us (8%)
  other arithmetic  18.4 us (6%)
  between operations  15 us (5%)
    all_to_all x1, waiting for transfers between devices, body(): lax.all_to_all(spread, ('xh', 'xl', 'z', 'c'), split_axis=0, concat_axis=...  69.6 us
    pallas_call x1, Pallas kernels, body(): pl.pallas_call(localize, grid=(group,), in_specs=[c_spec, whole(stencils)...  43.3 us
    ppermute x1, waiting for transfers between devices, body(): left = lax.ppermute(hi, ('xl', 'z'), up)  40.3 us
    unnamed x1, blocking collectives  24.7 us
    mul x6, local copies, waits for them, and re-layouts, row_stencils(): full = eye[None, :, None, None, :] * total[:, None, :, :, None]  20.6 us
    all_gather x1, waiting for transfers between devices, body(): ctrl = lax.all_gather(turned, ('xh', 'c'), axis=0)  19.3 us
    pallas_call x1, Pallas kernels, body(): pl.pallas_call(spread_kernel, grid=(members,), in_specs=[pl.BlockSpec((1,...  14 us
    all_to_all x1, starting transfers between devices, body(): lax.all_to_all(spread, ('xh', 'xl', 'z', 'c'), split_axis=0, concat_axis=...  12.3 us
  transfers between devices with their start and end apart: 6, of which 4 were waited for; matrix products, arithmetic and copies ran while one was open for 16% of the time, Pallas kernels for 13%

profile of v1, /device:TPU:2, one launch (start us, length us, event | category | flops | bytes accessed | tf_op | source)
XLA Modules:
  0.0 329.7 jit_solution(5229567939494894273)
XLA Ops:
  7.2 3.9 %copy.34 = bf16[1,20,128,4,128]{4,2,3,1,0:T(8,128)(2,1)} copy(bf16[1,20,128,4,128]{4,3,2,1,0:T(4,128)(2,1)} %param.12) | data formatting | bytes 5242880 | tf_op args[0]
  11.1 14.0 %shard_map.131 = bf16[2,16,2,5,4,16,128]{6,5,4,3,2,1,0:T(8,128)(2,1)} custom-call(bf16[20,4,128,128]{3,2,1,0:T(8,128)(2,1)} %bitcast.64, bf16[256,128]{1,0:T(8,128)(2,1)} %ci_ref.1), custom_call_target="tpu_custom_call" | custom-call | flops 671088640 | bytes 8000000 | tf_op jit(solution)/shard_map/pallas_call | solution.py:177
  25.1 12.3 %all-to-all-start = ((bf16[64,5,4,16,128]{4,3,2,1,0:T(8,128)(2,1)}), bf16[64,5,4,16,128]{4,3,2,1,0:T(8,128)(2,1)}, u32[]{:S(2)}, u32[]{:S(2)}) async-start(bf16[64,5,4,16,128]{4,3,2,1,0:T(8,128)(2,1)} %bitcast.63), calls=%async_computation | async-start | bytes 10485760 | tf_op jit(solution)/shard_map/all_to_all | solution.py:193
  37.5 0.9 convert_bitcast_fusion
  39.0 5.3 %mul.61 = bf16[16,16,16,10,16]{2,1,4,3,0:T(8,128)(2,1)} broadcast(bf16[16,16,10]{1,2,0:T(8,128)(2,1)S(1)} %fusion.11), dimensions={0,2,3} | broadcast | bytes 1315840 | tf_op jit(solution)/shard_map/mul | solution.py:106
  44.3 12.6 %mul.62 = bf16[16,256,160]{1,2,0:T(8,128)(2,1)S(1)} reshape(bf16[16,16,16,10,16]{2,1,4,3,0:T(8,128)(2,1)} %mul.61) | data formatting | bytes 2621440 | tf_op jit(solution)/shard_map/mul | solution.py:106
  56.9 1.8 copy.28
  59.7 1.5 broadcast_multiply_fusion.1.rest_0_
  61.2 19.3 %all-gather.4.cloned.1.call-done = bf16[32,256,128]{1,0,2:T(8,128)(2,1)} async-done(((bf16[8,256,128]{1,0,2:T(8,128)(2,1)}), bf16[32,256,128]{1,0,2:T(8,128)(2,1)}) %all-gather.4.cloned.1.call-update) | async-done | bytes 2097168 | tf_op jit(solution)/shard_map/all_gather | solution.py:197
  80.5 4.5 %copy.29 = bf16[32,256,128]{2,1,0:T(8,128)(2,1)} copy(bf16[32,256,128]{1,0,2:T(8,128)(2,1)} %all-gather.4.cloned.1.call-done) | data formatting | bytes 4194304 | tf_op jit(solution)/shard_map/all_gather | solution.py:197
  85.0 69.6 %all-to-all-done = bf16[64,5,4,16,128]{4,3,2,1,0:T(8,128)(2,1)} async-done(((bf16[64,5,4,16,128]{4,3,2,1,0:T(8,128)(2,1)}), bf16[64,5,4,16,128]{4,3,2,1,0:T(8,128)(2,1)}, u32[]{:S(2)}, u32[]{:S(2)}) %all-to-all-start) | async-done | bytes 5242912 | tf_op jit(solution)/shard_map/all_to_all | solution.py:193
  154.6 10.5 %shard_map.132 = (bf16[5,8,256,128]{3,2,1,0:T(8,128)(2,1)}, bf16[5,8,256,128]{3,2,1,0:T(8,128)(2,1)}) custom-call(bf16[2,32,5,4,16,128]{5,4,3,2,1,0:T(8,128)(2,1)} %bitcast.3.c_ref, bf16[16,256,160]{2,1,0:T(8,128)(2,1)} %broadcast_multiply_fusion.1.rest_0_, bf16[2,16,256,128]{3,2,1,0:T(8,128)(2,1)} %bitcast.66), custom_call_target="tpu_custom_call" | custom-call | tf_op jit(solution)/shard_map/pallas_call | solution.py:223
  165.1 2.5 collective-permute-start
  167.6 5.5 %collective-permute-start.1 = (bf16[5,8,256,128]{3,2,1,0:T(8,128)(2,1)}, bf16[5,8,256,128]{3,2,1,0:T(8,128)(2,1)}, u32[]{:S(2)}, u32[]{:S(2)}) collective-permute-start(bf16[5,8,256,128]{3,2,1,0:T(8,128)(2,1)} %get-tuple-element.4.rest_1_), channel_id=1, source_target_pairs={{8,0},{16,8},{24,16},{32,24},{40,32},{48,40},{56,48},{64,56},{72,6... | collective-permute-start | bytes 7864328 | tf_op jit(solution)/shard_map/ppermute | solution.py:235
  173.2 0.8 fusion
  174.5 0.8 broadcast_in_dim.107
  175.3 5.1 %all-to-all-start.2 = ((f32[8,1,6480]{2,1,0:T(1,128)}), f32[8,1,6480]{2,1,0:T(1,128)S(1)}, u32[]{:S(2)}, u32[]{:S(2)}) async-start(f32[8,1,6480]{2,1,0:T(1,128)} %broadcast_in_dim.107), calls=%async_computation.2 | async-start | bytes 417792 | tf_op jit(solution)/shard_map/all_to_all | solution.py:145
  180.4 3.0 all_gather.14
  183.8 4.2 %mul.67.rest_5_ = bf16[256,512]{1,0:T(8,128)(2,1)} reshape(bf16[16,16,32,16]{3,2,1,0:T(8,128)(2,1)S(1)} %broadcast_multiply_fusion) | data formatting | bytes 524288 | tf_op jit(solution)/shard_map/mul | solution.py:119
  188.0 0.7 copy.30
  188.7 40.3 %collective-permute-done.rest_3_ = bf16[5,8,256,128]{3,2,1,0:T(8,128)(2,1)} collective-permute-done((bf16[5,8,256,128]{3,2,1,0:T(8,128)(2,1)}, bf16[5,8,256,128]{3,2,1,0:T(8,128)(2,1)}, u32[]{:S(2)}, u32[]{:S(2)}) %collective-permute-start) | collective-permute-done | bytes 2621472 | tf_op jit(solution)/shard_map/ppermute | solution.py:234
  229.1 1.5 collective-permute-done.1.rest_4_
  230.6 43.3 %shard_map.133 = bf16[2,4,2,8,32,256]{5,4,3,2,1,0:T(8,128)(2,1)} custom-call(bf16[2,32,5,4,16,128]{5,4,3,2,1,0:T(8,128)(2,1)} %bitcast.3.c_ref, bf16[16,256,160]{2,1,0:T(8,128)(2,1)} %broadcast_multiply_fusion.1.rest_0_, bf16[5,8,256,128]{3,2,1,0:T(8,128)(2,1)} %get-tuple-element.4.rest_1_, bf16[5,8,256,128]{3,2,1,0:T(8,128)(2,1)} %get-tuple-element.5.rest_2_, ...), custom_call_target="tpu_custom_call" | custom-call | tf_op jit(solution)/shard_map/pallas_call | solution.py:237
  273.9 5.2 %all-to-all-start.1 = ((bf16[16,8,32,256]{3,2,1,0:T(8,128)(2,1)}), bf16[16,8,32,256]{3,2,1,0:T(8,128)(2,1)S(1)}, u32[]{:S(2)}, u32[]{:S(2)}) async-start(bf16[16,8,32,256]{3,2,1,0:T(8,128)(2,1)} %bitcast.65), calls=%async_computation.1 | async-start | bytes 4194304 | tf_op jit(solution)/shard_map/all_to_all | solution.py:255
  279.1 0.6 dynamic-slice
  280.8 7.3 %custom-call.9 = f32[1,80,80]{2,1,0:T(8,128)S(1)} custom-call(f32[1,80,80]{2,1,0:T(8,128)S(1)} %fusion.16), custom_call_target="Cholesky" | custom-call | tf_op jit(solution)/shard_map/jit(cholesky)/cholesky | solution.py:126
  288.2 0.6 compare_reduce_fusion
  288.8 0.7 fusion.13
  289.5 6.1 %custom-call.10 = f32[1,1,80,80]{2,3,1,0:T(8,128)S(1)} custom-call(f32[1,1,80,80]{3,2,1,0:T(8,128)S(1)} %fusion.13), custom_call_target="InvertDiagBlocksLowerTriangular" | custom-call | tf_op jit(solution)/shard_map/triangular_solve | solution.py:128
  296.1 24.7 %all-reduce.2 = f32[640]{0:T(1024)S(1)} all-reduce(f32[640]{0:T(1024)S(1)} %dynamic-update-slice.3), channel_id=3, replica_groups=mesh['xh'=2,'xl'=2,'z'=8,'c'=2,'y'=4] {'xh','y'}, use_global_device_ids=true, to_apply=%add.2 | all-reduce | flops 640 | bytes 5120
  320.9 0.7 reshape.245
  322.0 0.9 copy.32
  (59 shorter events, 3.7 us)
Async XLA Ops:
  25.1 12.4 %copy-start = (f32[1,128,8,256]{3,2,1,0:T(8,128)S(1)}, f32[1,128,8,256]{3,2,1,0:T(8,128)}, u32[]{:S(2)}) copy-start(f32[1,128,8,256]{3,2,1,0:T(8,128)} %param.15) | copy-start | bytes 3145732
  25.1 129.5 %all-to-all-start = ((bf16[64,5,4,16,128]{4,3,2,1,0:T(8,128)(2,1)}), bf16[64,5,4,16,128]{4,3,2,1,0:T(8,128)(2,1)}, u32[]{:S(2)}, u32[]{:S(2)}) async-start(bf16[64,5,4,16,128]{4,3,2,1,0:T(8,128)(2,1)} %bitcast.63), calls=%async_computation | async-start | bytes 10485760 | tf_op jit(solution)/shard_map/all_to_all | solution.py:193
  37.4 1.0 copy-start.5
  37.4 1.3 copy-start.7
  37.4 43.0 %all-gather.4.cloned.1.call-start = ((), (), s32[]{:S(2)}) async-start(), calls=%async_computation.3 | async-start | bytes 2621440 | tf_op jit(solution)/shard_map/all_gather | solution.py:197
  154.6 18.5 %copy-start.3 = (s32[1,2048]{1,0:T(1,128)S(1)}, s32[1,2048]{1,0:T(1,128)}, u32[]{:S(2)}) copy-start(s32[1,2048]{1,0:T(1,128)} %param.22) | copy-start | bytes 24580
  154.6 18.5 %copy-start.1 = (bf16[1,80,2048]{2,1,0:T(8,128)(2,1)S(1)}, bf16[1,80,2048]{2,1,0:T(8,128)(2,1)}, u32[]{:S(2)}) copy-start(bf16[1,80,2048]{2,1,0:T(8,128)(2,1)} %param.19) | copy-start | bytes 983044
  154.6 18.5 %copy-start.4 = (f32[1,2048]{1,0:T(1,128)S(1)}, f32[1,2048]{1,0:T(1,128)}, u32[]{:S(2)}) copy-start(f32[1,2048]{1,0:T(1,128)} %param.21) | copy-start | bytes 24580
  165.1 63.9 %collective-permute-start = (bf16[5,8,256,128]{3,2,1,0:T(8,128)(2,1)}, bf16[5,8,256,128]{3,2,1,0:T(8,128)(2,1)}, u32[]{:S(2)}, u32[]{:S(2)}) collective-permute-start(bf16[5,8,256,128]{3,2,1,0:T(8,128)(2,1)} %get-tuple-element.5.rest_2_), channel_id=1, source_target_pairs={{0,8},{8,16},{16,24},{24,32},{32,40},{40,48},{48,56},{56,64},{64,7... | collective-permute-start | bytes 7864328 | tf_op jit(solution)/shard_map/ppermute | solution.py:234
  167.6 63.0 %collective-permute-start.1 = (bf16[5,8,256,128]{3,2,1,0:T(8,128)(2,1)}, bf16[5,8,256,128]{3,2,1,0:T(8,128)(2,1)}, u32[]{:S(2)}, u32[]{:S(2)}) collective-permute-start(bf16[5,8,256,128]{3,2,1,0:T(8,128)(2,1)} %get-tuple-element.4.rest_1_), channel_id=1, source_target_pairs={{8,0},{16,8},{24,16},{32,24},{40,32},{48,40},{56,48},{64,56},{72,6... | collective-permute-start | bytes 7864328 | tf_op jit(solution)/shard_map/ppermute | solution.py:235
  173.2 1.0 copy-start.8
  174.0 6.4 %copy-start.6 = (bf16[8,24]{1,0:T(8,128)(2,1)S(1)}, bf16[8,24]{1,0:T(8,128)(2,1)}, u32[]{:S(2)}) copy-start(bf16[8,24]{1,0:T(8,128)(2,1)} %param.16) | copy-start | bytes 1156
  175.3 98.6 %all-to-all-start.2 = ((f32[8,1,6480]{2,1,0:T(1,128)}), f32[8,1,6480]{2,1,0:T(1,128)S(1)}, u32[]{:S(2)}, u32[]{:S(2)}) async-start(f32[8,1,6480]{2,1,0:T(1,128)} %broadcast_in_dim.107), calls=%async_computation.2 | async-start | bytes 417792 | tf_op jit(solution)/shard_map/all_to_all | solution.py:145
  183.6 4.5 %copy-start.2 = (bf16[128,128]{1,0:T(8,128)(2,1)S(1)}, bf16[128,128]{1,0:T(8,128)(2,1)}, u32[]{:S(2)}) copy-start(bf16[128,128]{1,0:T(8,128)(2,1)} %param.18) | copy-start | bytes 98308
  273.9 5.2 %copy-start.9 = (u32[256]{0:T(256)S(1)}, u32[256]{0:T(256)}, u32[]{:S(2)}) copy-start(u32[256]{0:T(256)} %constant.102) | copy-start | bytes 3076
  273.9 47.6 %all-to-all-start.1 = ((bf16[16,8,32,256]{3,2,1,0:T(8,128)(2,1)}), bf16[16,8,32,256]{3,2,1,0:T(8,128)(2,1)S(1)}, u32[]{:S(2)}, u32[]{:S(2)}) async-start(bf16[16,8,32,256]{3,2,1,0:T(8,128)(2,1)} %bitcast.65), calls=%async_computation.1 | async-start | bytes 4194304 | tf_op jit(solution)/shard_map/all_to_all | solution.py:255
Sparse Core Ops, SparseCore 0:
  40.0 40.3 all-gather.3

commit v2 on v1

v2 whole, which is shorter than its diff:
```python
import functools

import jax
import jax.numpy as jnp
from jax import lax
from jax.experimental import pallas as pl
from jax.experimental.pallas import tpu as pltpu
from jax.sharding import Mesh, PartitionSpec as P

NREG = 8
BF = jnp.bfloat16
F32 = jnp.float32
GR = 16
WIN = 10


def from_everyone(value, axes):
    copies = jnp.broadcast_to(value, (lax.axis_size(axes), *value.shape))
    return lax.all_to_all(copies, axes, split_axis=0, concat_axis=0, tiled=True)


MESH = pl.DeviceIdType.MESH


def one_hot(shape, of_row, of_col):
    row = lax.broadcasted_iota(jnp.int32, shape, 0)
    col = lax.broadcasted_iota(jnp.int32, shape, 1)
    return (of_row(row) == of_col(col)).astype(BF)


def window_start(group, coarse_rows):
    return min(max(group * GR // 2 - 1, 0), coarse_rows - WIN)


def main_kernel(sizes, refs):
    nxh, nxl, nz, nc, ny, scale = sizes
    x_ref, ci_ref, rwt_ref, cq_ref, band_ref, row_ref, lev_ref, o_ref, *refs = refs
    perm, sent, land, sten, stage, ctrl, bands, bandf, field, halo, fine, banded, acc, *refs = refs
    parts, sums, total, moved, *sems = refs
    (s_go, s_in, h_go, h_in, c_go, c_in, f_go, f_in, b_go, b_in, p_go, p_in, m_go, m_in) = sems

    nk, ndest, own_rows, cols, lev = sent.shape
    coarse = land.shape[2]
    groups = sten.shape[0]
    half = cols // 2
    blocks = nz * nc
    xh, xl, z, c, y = (lax.axis_index(a) for a in ("xh", "xl", "z", "c", "y"))
    block = z * nc + c
    tile = xl * blocks + block
    me = (xh * nxl + xl) * blocks + block
    team = (xh * nxl + xl) * ny + y

    def at_dest(d):
        m, b = d // blocks, d % blocks
        return {"xh": m // nxl, "xl": m % nxl, "z": b // nc, "c": b % nc}

    def at_team(p):
        m = p // ny
        return {"xh": m // nxl, "xl": m % nxl, "y": p % ny}

    barrier = pltpu.get_barrier_semaphore()

    def greet(n, carry):
        pl.semaphore_signal(
            barrier, inc=1, device_id=at_dest((me + n) % ndest), device_id_type=MESH
        )
        return carry

    lax.fori_loop(1, ndest, greet, 0)
    nteam = nxh * nxl * ny

    def greet_team(n, carry):
        p = (team + n) % nteam

        @pl.when(p % ny != y)
        def _():
            pl.semaphore_signal(barrier, inc=1, device_id=at_team(p), device_id_type=MESH)

        return carry

    lax.fori_loop(1, nteam, greet_team, 0)

    flat = own_rows * lev
    perm[...] = one_hot(
        (flat, flat), lambda p: (p % lev) * own_rows + p // lev, lambda q: q
    )

    def spread(k, carry):
        def group_of(m, carry):
            by_row = jnp.dot(
                perm[...], x_ref[m * nk + k], preferred_element_type=F32
            ).astype(BF)
            out = lax.dot_general(
                ci_ref[...], by_row, (((1,), (1,)), ((), ())), preferred_element_type=F32
            ).astype(BF)
            for i in range(own_rows):
                sent[k, pl.ds(m * blocks, blocks), i] = out[:, i * lev : (i + 1) * lev].reshape(
                    blocks, cols, lev
                )
            return carry

        return lax.fori_loop(0, nxh * nxl, group_of, carry)

    def send(k):
        def one(n, carry):
            d = (me + n) % ndest
            pltpu.make_async_remote_copy(
                src_ref=sent.at[k, d],
                dst_ref=land.at[k, xh, pl.ds(tile * own_rows, own_rows)],
                send_sem=s_go.at[k],
                recv_sem=s_in.at[k],
                device_id=at_dest(d),
                device_id_type=MESH,
            ).start()
            return carry

        lax.fori_loop(1, ndest, one, 0)
        land[k, xh, pl.ds(tile * own_rows, own_rows)] = sent[k, me]

    def wait_bytes(ref, sem):
        pltpu.make_async_copy(ref, ref, sem).wait()

    spread(0, 0)
    pl.semaphore_wait(barrier, ndest - 1 + nteam - nxh * nxl)

    to_xl, to_z, to_c = c, (xl * nz + z) // nc, (xl * nz + z) % nc
    home = (to_xl == xl) & (to_z == z) & (to_c == c)
    quarter = pltpu.make_async_remote_copy(
        src_ref=cq_ref,
        dst_ref=stage,
        send_sem=c_go,
        recv_sem=c_in,
        device_id={"xl": to_xl, "z": to_z, "c": to_c},
        device_id_type=MESH,
    )

    @pl.when(jnp.logical_not(home))
    def _():
        quarter.start()

    @pl.when(home)
    def _():
        stage[...] = cq_ref[...]

    for side in range(nxl):
        here = (to_z == z) & (to_c == c) & (xl == side)

        @pl.when(jnp.logical_not(here))
        def _():
            pltpu.make_async_remote_copy(
                src_ref=band_ref,
                dst_ref=bands.at[c],
                send_sem=b_go.at[side],
                recv_sem=b_in.at[c],
                device_id={"xl": side, "z": to_z, "c": to_c},
                device_id_type=MESH,
            ).start()

        @pl.when(here)
        def _():
            bands[c] = band_ref[...]

    send(0)
    spread(1, 0)
    send(1)

    @pl.when(jnp.logical_not(home))
    def _():
        quarter.wait()

    quarter_cols = cq_ref.shape[0]
    slot = xh * cols + xl * half + y * quarter_cols

    def forward(n, carry):
        p = (team + n) % nteam
        pltpu.make_async_remote_copy(
            src_ref=stage,
            dst_ref=ctrl.at[pl.ds(slot, quarter_cols)],
            send_sem=f_go,
            recv_sem=f_in,
            device_id=at_team(p),
            device_id_type=MESH,
        ).start()
        return carry

    lax.fori_loop(1, nteam, forward, 0)
    ctrl[pl.ds(slot, quarter_cols)] = stage[...]
    lax.fori_loop(2, nk, spread, 0)

    span = WIN * cols
    p_id = lax.broadcasted_iota(jnp.int32, (cols * GR, span), 0)
    q_id = lax.broadcasted_iota(jnp.int32, (cols * GR, span), 1)
    same = q_id % cols == p_id // GR

    def stencil(g, carry):
        take = (
            lax.broadcasted_iota(jnp.int32, (cols * GR, groups * GR), 1)
            == lax.broadcasted_iota(jnp.int32, (cols * GR, groups * GR), 0) % GR + g * GR
        ).astype(BF)
        w = jnp.dot(take, rwt_ref[...], preferred_element_type=F32)
        start = jnp.minimum(jnp.maximum(g * (GR // 2) - 1, 0), coarse - WIN)
        full = jnp.zeros((cols * GR, span), F32)
        for s in range(3):
            wanted = g * (GR // 2) - start + (p_id % GR) // 2 + s - 1
            full = jnp.where(same & (q_id // cols == wanted), w[:, s : s + 1], full)
        sten[g] = full.astype(BF)
        return carry

    lax.fori_loop(0, groups, stencil, 0)

    for side in range(2):
        here = (xl == block // nz) & (z == block % nz) & (c == side)

        @pl.when(jnp.logical_not(here))
        def _():
            wait_bytes(bands.at[side], b_in.at[side])

    narrow = jnp.concatenate(
        [bands[0], pltpu.roll(bands[1], half, 1)], axis=0
    ).astype(BF)
    wide_src = 4 * half * GR
    take_src = one_hot((narrow.shape[1], wide_src), lambda m: m, lambda q: q // GR)
    take_col = one_hot((cols * GR, cols), lambda p: p // GR, lambda j: j)
    wide = jnp.dot(narrow, take_src, preferred_element_type=F32).astype(BF)
    full = jnp.dot(take_col, wide, preferred_element_type=F32)
    p_id2 = lax.broadcasted_iota(jnp.int32, full.shape, 0)
    q_id2 = lax.broadcasted_iota(jnp.int32, full.shape, 1)
    bandf[...] = jnp.where(p_id2 % GR == q_id2 % GR, full, 0.0).astype(BF)

    acc[...] = jnp.zeros_like(acc)

    def refine_group(k, group):
        start = window_start(group, coarse)
        windows = [land[k, t, pl.ds(start, WIN)].reshape(WIN * cols, lev) for t in range(2)]
        out = jnp.dot(
            sten[group], jnp.concatenate(windows, axis=1), preferred_element_type=F32
        ).astype(BF)
        return [out[:, t * lev : (t + 1) * lev].reshape(cols, GR, lev) for t in range(2)]

    def project(k):
        for group in range(groups):
            rows = pl.ds(group * GR, GR)
            first, second = refine_group(k, group)
            both = first.astype(F32) * ctrl[pl.ds(0, cols), rows, :].astype(F32)
            both = both + second.astype(F32) * ctrl[pl.ds(cols, cols), rows, :].astype(F32)
            both = both.astype(BF)
            field[k, 0, :, rows, :] = both[:half]
            field[k, 1, :, rows, :] = both[half:]

    def halo_copy(k, side):
        other = block + 1 if side == 0 else block - 1
        return pltpu.make_async_remote_copy(
            src_ref=field.at[k, 1 - side],
            dst_ref=halo.at[k, side],
            send_sem=h_go.at[k, side],
            recv_sem=h_in.at[k, side],
            device_id={"z": other // nc, "c": other % nc},
            device_id_type=MESH,
        )

    sends = (block < blocks - 1, block > 0)
    gets = (block > 0, block < blocks - 1)

    def localize(k):
        for side in range(2):

            @pl.when(gets[side])
            def _():
                wait_bytes(halo.at[k, side], h_in.at[k, side])

            @pl.when(jnp.logical_not(gets[side]))
            def _():
                halo[k, side] = jnp.zeros(halo.shape[2:], BF)

        for group in range(groups):
            rows = pl.ds(group * GR, GR)
            for t, part in enumerate(refine_group(k, group)):
                fine[t, :, rows, :] = part
        for group in range(0, groups, 2):
            sides = []
            for g in (group, group + 1):
                rows = pl.ds(g * GR, GR)
                pieces = [
                    ref[:, rows, :].reshape(half * GR, lev)
                    for ref in (halo.at[k, 0], field.at[k, 0], field.at[k, 1], halo.at[k, 1])
                ]
                sides.append(jnp.concatenate(pieces, axis=0))
            mixed = jnp.dot(
                bandf[...], jnp.concatenate(sides, axis=1), preferred_element_type=F32
            ).astype(BF)
            for n, g in enumerate((group, group + 1)):
                banded[:, pl.ds(g * GR, GR), :] = mixed[:, n * lev : (n + 1) * lev].reshape(
                    cols, GR, lev
                )
        for j in range(0, cols, 2):
            pair = jnp.concatenate([banded[j], banded[j + 1]], axis=1)
            mixed = jnp.dot(row_ref[...], pair, preferred_element_type=F32).astype(BF)
            local = jnp.dot(mixed, lev_ref[...], preferred_element_type=F32)
            for n in range(2):
                part = local[:, n * lev : (n + 1) * lev]
                for t in range(2):
                    acc[t, j + n] += fine[t, j + n].astype(F32) * part

    def wait_all_but_one(k, sem):
        wait_bytes(sent.at[k, pl.ds(0, ndest - 1)], sem.at[k])

    def step(k, carry):
        @pl.when(k < nk)
        def _():
            wait_all_but_one(k, s_in)

            @pl.when(k == 0)
            def _():
                wait_bytes(ctrl.at[pl.ds(0, (nteam - 1) * quarter_cols)], f_in)

            project(k)
            for side in range(2):

                @pl.when(sends[side])
                def _():
                    halo_copy(k, side).start()

            @pl.when(k + 2 < nk)
            def _():
                send(k + 2)

        @pl.when(k >= 1)
        def _():
            localize(k - 1)

        return carry

    lax.fori_loop(0, nk + 1, step, 0)

    nl, ll = ny, lev // ny

    def flip(j, carry):
        for t in range(2):
            turned = acc[t, j].T.astype(BF)
            for q in range(nl):
                parts[(t * nxl + j // half) * ny + q, j % half] = turned[q * ll : (q + 1) * ll]
        return carry

    lax.fori_loop(0, cols, flip, 0)

    def hand_over(n, carry):
        p = (team + n) % nteam
        pltpu.make_async_remote_copy(
            src_ref=parts.at[p],
            dst_ref=sums.at[team],
            send_sem=p_go,
            recv_sem=p_in,
            device_id=at_team(p),
            device_id_type=MESH,
        ).start()
        return carry

    lax.fori_loop(1, nteam, hand_over, 0)
    sums[team] = parts[team]
    wait_bytes(sums.at[pl.ds(0, nteam - 1)], p_in)
    for j in range(half):
        value = sums[0, j].astype(F32)
        for p in range(1, nteam):
            value = value + sums[p, j].astype(F32)
        total[j] = value * scale

    from_c, from_block = xl, (z * nc + c)
    dest = (tile * 2) % (blocks * nxl) + xl
    d_block = dest % blocks
    stays = dest == tile
    move = pltpu.make_async_remote_copy(
        src_ref=total,
        dst_ref=moved,
        send_sem=m_go,
        recv_sem=m_in,
        device_id={"xl": dest // blocks, "z": d_block // nc, "c": d_block % nc},
        device_id_type=MESH,
    )

    @pl.when(jnp.logical_not(stays))
    def _():
        move.start()

    @pl.when(stays)
    def _():
        moved[...] = total[...]

    def left(k, carry):
        wait_all_but_one(k, s_go)
        for side in range(2):

            @pl.when(sends[side])
            def _():
                wait_bytes(field.at[k, side], h_go.at[k, side])

        return carry

    lax.fori_loop(0, nk, left, 0)
    wait_bytes(ctrl.at[pl.ds(0, (nteam - 1) * quarter_cols)], f_go)
    wait_bytes(sums.at[pl.ds(0, nteam - 1)], p_go)
    for side in range(nxl):
        here = (to_z == z) & (to_c == c) & (xl == side)

        @pl.when(jnp.logical_not(here))
        def _():
            wait_bytes(bands.at[side], b_go.at[side])

    @pl.when(jnp.logical_not(stays))
    def _():
        move.wait()

    o_ref[...] = moved[...]


def solve_weights(gram_sums, right_side):
    member_count = gram_sums.shape[-1]
    system = gram_sums + (member_count - 1) * jnp.eye(member_count, dtype=F32)
    factor = jnp.linalg.cholesky(system)
    halfway = lax.linalg.triangular_solve(factor, right_side[..., None], left_side=True, lower=True)
    result = lax.linalg.triangular_solve(
        factor, halfway, left_side=True, lower=True, transpose_a=True
    )
    return result[..., 0]


def letkf(hx_pert, innov, obs_prec, obs_region):
    observed = hx_pert[0]
    members = observed.shape[0]
    weighted = (observed * obs_prec[0][None, :]).astype(BF)
    labels = lax.broadcasted_iota(jnp.int32, (NREG, observed.shape[1]), 0)
    member_of = obs_region[0][None, :] == labels
    masked = jnp.where(member_of[:, None, :], weighted[None], jnp.zeros((), BF))
    gram = jnp.einsum("rko,jo->rkj", masked, observed, preferred_element_type=F32)
    innov_rows = jnp.where(member_of, innov[0][None, :], 0.0)
    right = jnp.dot(innov_rows, weighted.astype(F32).T)
    packed = jnp.concatenate([gram.reshape(NREG, -1), right], axis=1)
    arrived = lax.all_to_all(packed[:, None], ("xh", "y"), split_axis=0, concat_axis=0, tiled=True)
    total = jnp.sum(arrived, axis=0)
    size = members * members
    own = solve_weights(total[:, :size].reshape(-1, members, members), total[:, size:])
    everyone = from_everyone(own, ("xh", "y"))
    return everyone.reshape(NREG, members)


def body(
    ens_coarse,
    col_interp,
    row_weights,
    ctrl_vec,
    band_loc,
    row_loc,
    level_loc,
    hx_pert,
    innov,
    obs_prec,
    obs_region,
):
    nxh, nxl, nz, nc, ny = (lax.axis_size(a) for a in ("xh", "xl", "z", "c", "y"))
    _, members, lev, own_rows, coarse_cols = ens_coarse.shape
    fine_cols = col_interp.shape[0]
    fine_rows = row_weights.shape[1]
    blocks = nz * nc
    cols = fine_cols // blocks
    half = cols // 2
    group = members // (nxh * nxl)
    tiles = nxl * blocks
    coarse = tiles * own_rows
    total_members = hx_pert.shape[1]
    nteam = nxh * nxl * ny
    quarter = half // ny

    x = ens_coarse.reshape(members, lev * own_rows, coarse_cols)
    rwt = jnp.pad(row_weights.T, ((0, 0), (0, 125)))
    mine = lax.dynamic_slice_in_dim(ctrl_vec[0], lax.axis_index("y") * quarter, quarter, 1)
    mine = jnp.transpose(mine.astype(BF), (1, 2, 0))
    band = jnp.pad(band_loc.astype(F32), ((0, 0), (0, 128 - band_loc.shape[1])))
    none = jnp.zeros_like(level_loc)
    lev_two = jnp.block([[level_loc.T, none], [none, level_loc.T]])

    vm = pl.BlockSpec(memory_space=pltpu.VMEM)
    dma = pltpu.SemaphoreType.DMA
    increment = pl.pallas_call(
        lambda *refs: main_kernel((nxh, nxl, nz, nc, ny, 1.0 / (total_members - 1)), refs),
        in_specs=[vm] * 7,
        out_specs=vm,
        out_shape=jax.ShapeDtypeStruct((half, lev // ny, fine_rows), F32),
        scratch_shapes=[
            pltpu.VMEM((own_rows * lev, own_rows * lev), BF),
            pltpu.VMEM((group, nxh * tiles, own_rows, cols, lev), BF),
            pltpu.VMEM((group, nxh, coarse, cols, lev), BF),
            pltpu.VMEM((fine_rows // GR, cols * GR, WIN * cols), BF),
            pltpu.VMEM((quarter, fine_rows, lev), BF),
            pltpu.VMEM((nxh * cols, fine_rows, lev), BF),
            pltpu.VMEM((2, *band.shape), F32),
            pltpu.VMEM((cols * GR, 4 * half * GR), BF),
            pltpu.VMEM((group, 2, half, fine_rows, lev), BF),
            pltpu.VMEM((group, 2, half, fine_rows, lev), BF),
            pltpu.VMEM((nxh, cols, fine_rows, lev), BF),
            pltpu.VMEM((cols, fine_rows, lev), BF),
            pltpu.VMEM((nxh, cols, fine_rows, lev), F32),
            pltpu.VMEM((nteam, half, lev // ny, fine_rows), BF),
            pltpu.VMEM((nteam, half, lev // ny, fine_rows), BF),
            pltpu.VMEM((half, lev // ny, fine_rows), F32),
            pltpu.VMEM((half, lev // ny, fine_rows), F32),
            dma((group,)),
            dma((group,)),
            dma((group, 2)),
            dma((group, 2)),
            dma,
            dma,
            dma,
            dma,
            dma((2,)),
            dma((2,)),
            dma,
            dma,
            dma,
            dma,
        ],
        compiler_params=pltpu.CompilerParams(
            collective_id=0, has_side_effects=True, vmem_limit_bytes=62 << 20
        ),
    )(x, col_interp, rwt, mine, band, row_loc, lev_two)
    increment = jnp.transpose(increment, (1, 0, 2))
    weights = letkf(hx_pert, innov, obs_prec, obs_region)
    return (increment[None], weights)


def solution(mesh):
    shape = (2, 2, mesh.shape["tile"] // 4, 2, mesh.shape["mem"])
    fine_mesh = Mesh(mesh.devices.reshape(shape), ("xh", "xl", "z", "c", "y"))
    tile = ("xl", "z", "c")
    obs = (*tile, "y")
    placed = (
        P("xh", "y", None, tile, None),
        P(),
        P(),
        P("xh", None, tile, None),
        P(tile, None),
        P(),
        P(),
        P("xh", None, obs),
        P("xh", obs),
        P("xh", obs),
        P("xh", obs),
    )
    return jax.shard_map(
        body,
        mesh=fine_mesh,
        in_specs=placed,
        out_specs=(P("xh", "y", tile, None), P(tile, None)),
        check_vma=False,
    )
```

time: 332 us -> 269 us (0.81)
  the two profiles are of different devices: /device:TPU:2 before, /device:TPU:94 now
where the time goes in v2:
time: 269 us; the launch traced here: 268 us
  Pallas kernels  223 us (83%)
  other arithmetic  18.1 us (7%)
  starting transfers between devices  14.5 us (5%)
  local copies, waits for them, and re-layouts  6.1 us (2%)
  waiting for transfers between devices  3.41 us (1%)
    pallas_call x1, Pallas kernels, body(): pl.pallas_call(lambda *refs: main_kernel((nxh, nxl, nz, nc, ny, 1.0 / (to...  223 us
    another operation x3, other arithmetic, solve_weights(): factor = jnp.linalg.cholesky(system)  7.98 us
    all_to_all x1, starting transfers between devices, from_everyone(): return lax.all_to_all(copies, axes, split_axis=0, concat_axis=0, tiled=True)  7.46 us
    all_to_all x1, starting transfers between devices, letkf(): lax.all_to_all(packed[:, None], ('xh', 'y'), split_axis=0, concat_axis=0,...  7.09 us
    another operation x2, other arithmetic, solve_weights(): lax.linalg.triangular_solve(factor, halfway, left_side=True, lower=True,...  6.78 us
  transfers between devices with their start and end apart: 2, of which 1 were waited for; matrix products, arithmetic and copies ran while one was open for 2% of the time, Pallas kernels for 83%

profile of v2, /device:TPU:94, one launch (start us, length us, event | category | flops | bytes accessed | tf_op | source)
XLA Modules:
  0.0 268.4 jit_solution(3800771409398293717)
XLA Ops:
  0.6 0.0 copy-start
  0.6 0.8 iota_compare_fusion.2
  1.4 1.0 fusion.5
  2.5 0.0 copy-start.3
  2.5 1.8 fusion
  4.4 0.2 reshape.121
  4.6 0.2 fusion.6
  4.8 0.8 broadcast_in_dim.62
  5.7 7.1 %all-to-all-start = ((f32[8,1,6480]{2,1,0:T(1,128)}), f32[8,1,6480]{2,1,0:T(1,128)S(1)}, u32[]{:S(2)}, u32[]{:S(2)}) async-start(f32[8,1,6480]{2,1,0:T(1,128)} %broadcast_in_dim.62), calls=%async_computation | async-start | bytes 417792 | tf_op jit(solution)/shard_map/all_to_all | solution.py:437
  12.8 0.1 copy.20
  12.9 0.7 fusion.12.refs_6_
  13.6 0.1 constant_dynamic-slice_fusion
  13.7 3.4 %all-to-all-done = f32[8,1,6480]{2,1,0:T(1,128)S(1)} async-done(((f32[8,1,6480]{2,1,0:T(1,128)}), f32[8,1,6480]{2,1,0:T(1,128)S(1)}, u32[]{:S(2)}, u32[]{:S(2)}) %all-to-all-start) | async-done | bytes 207392 | tf_op jit(solution)/shard_map/all_to_all | solution.py:437
  17.1 0.2 reduce_sum.11
  17.3 0.1 slice_reduce_fusion
  17.4 0.1 reshape.122
  17.5 0.1 copy.21
  17.6 7.3 %custom-call.9 = f32[1,80,80]{2,1,0:T(8,128)S(1)} custom-call(f32[1,80,80]{2,1,0:T(8,128)S(1)} %fusion.17), custom_call_target="Cholesky" | custom-call | tf_op jit(solution)/shard_map/jit(cholesky)/cholesky | solution.py:418
  24.9 0.6 compare_reduce_fusion
  25.6 0.7 fusion.14
  26.2 6.1 %custom-call.10 = f32[1,1,80,80]{2,3,1,0:T(8,128)S(1)} custom-call(f32[1,1,80,80]{3,2,1,0:T(8,128)S(1)} %fusion.14), custom_call_target="InvertDiagBlocksLowerTriangular" | custom-call | tf_op jit(solution)/shard_map/triangular_solve | solution.py:420
  32.4 0.1 convolution_bitcast_fusion.1
  32.5 0.2 convolution_bitcast_fusion
  32.7 0.6 broadcast_in_dim.63
  33.3 7.5 %all-to-all-start.1 = ((f32[8,1,80]{2,1,0:T(1,128)}), f32[8,1,80]{2,1,0:T(1,128)S(1)}, u32[]{:S(2)}, u32[]{:S(2)}) async-start(f32[8,1,80]{2,1,0:T(1,128)} %broadcast_in_dim.63), calls=%async_computation.1 | async-start | bytes 8192 | tf_op jit(solution)/shard_map/all_to_all | solution.py:19
  40.8 0.6 pad_convert_fusion.refs_4_
  41.3 0.8 copy.23
  42.1 0.1 copy.18
  42.3 0.6 pad.12.refs_2_
  42.9 223.0 %shard_map.122 = f32[8,32,256]{2,1,0:T(8,128)} custom-call(bf16[20,512,128]{2,1,0:T(8,128)(2,1)} %bitcast.46, bf16[256,128]{1,0:T(8,128)(2,1)} %refs_1_.1, bf16[256,128]{1,0:T(8,128)(2,1)} %pad.12.refs_2_, bf16[2,256,128]{2,1,0:T(8,128)(2,1)} %bitcast.48, f32[8,128]{1,0:T(8,128)} %pad_convert_fusion.refs_4_, bf16[256,256]{1,0:T(8,128)(2,1)} %refs_5_.1, ...), custom_call_target="tpu_custom_call" | custom-call | tf_op jit(solution)/shard_map/pallas_call | solution.py:482
  266.0 1.8 copy.22
  267.8 0.6 copy.25
  (20 shorter events, 0.2 us)
Async XLA Ops:
  0.6 12.9 %copy-start = (f32[1,128,8,256]{3,2,1,0:T(8,128)S(1)}, f32[1,128,8,256]{3,2,1,0:T(8,128)}, u32[]{:S(2)}) copy-start(f32[1,128,8,256]{3,2,1,0:T(8,128)} %param.14) | copy-start | bytes 3145732
  2.5 2.1 copy-start.1
  2.5 2.1 copy-start.3
  2.5 2.1 copy-start.4
  2.5 2.1 copy-start.7
  2.5 10.2 %copy-start.2 = (bf16[128,128]{1,0:T(8,128)(2,1)S(1)}, bf16[128,128]{1,0:T(8,128)(2,1)}, u32[]{:S(2)}) copy-start(bf16[128,128]{1,0:T(8,128)(2,1)} %param.17) | copy-start | bytes 98308
  4.4 36.4 %copy-start.5 = (bf16[8,24]{1,0:T(8,128)(2,1)S(1)}, bf16[8,24]{1,0:T(8,128)(2,1)}, u32[]{:S(2)}) copy-start(bf16[8,24]{1,0:T(8,128)(2,1)} %param.15) | copy-start | bytes 1156
  4.4 37.7 %copy-start.6 = (bf16[3,256]{1,0:T(4,128)(2,1)S(1)}, bf16[3,256]{1,0:T(4,128)(2,1)}, u32[]{:S(2)}) copy-start(bf16[3,256]{1,0:T(4,128)(2,1)} %param.13) | copy-start | bytes 4612
  5.7 11.4 %all-to-all-start = ((f32[8,1,6480]{2,1,0:T(1,128)}), f32[8,1,6480]{2,1,0:T(1,128)S(1)}, u32[]{:S(2)}, u32[]{:S(2)}) async-start(f32[8,1,6480]{2,1,0:T(1,128)} %broadcast_in_dim.62), calls=%async_computation | async-start | bytes 417792 | tf_op jit(solution)/shard_map/all_to_all | solution.py:437
  33.3 234.5 %all-to-all-start.1 = ((f32[8,1,80]{2,1,0:T(1,128)}), f32[8,1,80]{2,1,0:T(1,128)S(1)}, u32[]{:S(2)}, u32[]{:S(2)}) async-start(f32[8,1,80]{2,1,0:T(1,128)} %broadcast_in_dim.63), calls=%async_computation.1 | async-start | bytes 8192 | tf_op jit(solution)/shard_map/all_to_all | solution.py:19

commit v3 on v2

--- a/solution.py
+++ b/solution.py
@@ -14,11 +14,6 @@
 WIN = 10
 
 
-def from_everyone(value, axes):
-    copies = jnp.broadcast_to(value, (lax.axis_size(axes), *value.shape))
-    return lax.all_to_all(copies, axes, split_axis=0, concat_axis=0, tiled=True)
-
-
 MESH = pl.DeviceIdType.MESH
 
 
@@ -34,10 +29,12 @@
 
 def main_kernel(sizes, refs):
     nxh, nxl, nz, nc, ny, scale = sizes
-    x_ref, ci_ref, rwt_ref, cq_ref, band_ref, row_ref, lev_ref, o_ref, *refs = refs
+    x_ref, ci_ref, rwt_ref, cq_ref, band_ref, row_ref, lev_ref, *refs = refs
+    hx_ref, innov_ref, prec_ref, region_ref, o_ref, w_ref, *refs = refs
     perm, sent, land, sten, stage, ctrl, bands, bandf, field, halo, fine, banded, acc, *refs = refs
-    parts, sums, total, moved, *sems = refs
-    (s_go, s_in, h_go, h_in, c_go, c_in, f_go, f_in, b_go, b_in, p_go, p_in, m_go, m_in) = sems
+    parts, sums, total, moved, gram, grams, system, answer, answers, *sems = refs
+    s_go, s_in, h_go, h_in, c_go, c_in, f_go, f_in, b_go, b_in, p_go, p_in, m_go, m_in, *sems = sems
+    g_go, g_in, w_go, w_in = sems
 
     nk, ndest, own_rows, cols, lev = sent.shape
     coarse = land.shape[2]
@@ -185,6 +182,79 @@
 
     lax.fori_loop(1, nteam, forward, 0)
     ctrl[pl.ds(slot, quarter_cols)] = stage[...]
+    members, obs = hx_ref.shape
+    lanes = gram.shape[2]
+    region = xh * ny + y
+    nregion = nxh * ny
+
+    def at_region(g):
+        return {"xh": g // ny, "y": g % ny}
+
+    weighted = (hx_ref[...].astype(F32) * prec_ref[...]).astype(BF)
+    padded = jnp.concatenate([hx_ref[...], jnp.zeros((lanes - members, obs), BF)], axis=0)
+    lane = lax.broadcasted_iota(jnp.int32, (members, lanes), 1)
+    row_of = lax.broadcasted_iota(jnp.int32, (members, lanes), 0)
+    for g in range(nregion):
+        inside = region_ref[...] == g
+        masked = jnp.where(inside, weighted.astype(F32), 0.0)
+        right = jnp.sum(masked * innov_ref[...], axis=1, keepdims=True)
+        product = lax.dot_general(
+            masked.astype(BF), padded, (((1,), (1,)), ((), ())), preferred_element_type=F32
+        )
+        gram[g] = jnp.where(lane == members, right, product)
+
+    def hand_gram(n, carry):
+        g = (region + n) % nregion
+        pltpu.make_async_remote_copy(
+            src_ref=gram.at[g],
+            dst_ref=grams.at[region],
+            send_sem=g_go,
+            recv_sem=g_in,
+            device_id=at_region(g),
+            device_id_type=MESH,
+        ).start()
+        return carry
+
+    lax.fori_loop(1, nregion, hand_gram, 0)
+    grams[region] = gram[region]
+
+    def gather_system():
+        wait_bytes(grams.at[pl.ds(0, nregion - 1)], g_in)
+        value = grams[0]
+        for g in range(1, nregion):
+            value = value + grams[g]
+        system[...] = value + jnp.where(lane == row_of, members - 1.0, 0.0)
+
+    def eliminate(j, carry):
+        value = system[...]
+        pivot_row = system[pl.ds(j, 1), :]
+        column = jnp.sum(jnp.where(lane == j, value, 0.0), axis=1, keepdims=True)
+        pivot = jnp.sum(jnp.where(lane[:1] == j, pivot_row, 0.0), axis=1, keepdims=True)
+        scaled = pivot_row / pivot
+        system[...] = jnp.where(row_of == j, scaled, value - column * scaled)
+        return carry
+
+    def hand_answer():
+        solved = jnp.sum(
+            jnp.where(lane == members, system[...], 0.0), axis=1, keepdims=True
+        )
+        across = jnp.sum(jnp.where(lane == row_of, solved, 0.0), axis=0, keepdims=True)
+        answer[...] = jnp.broadcast_to(across, answer.shape)
+
+        def one(n, carry):
+            pltpu.make_async_remote_copy(
+                src_ref=answer,
+                dst_ref=answers.at[region],
+                send_sem=w_go,
+                recv_sem=w_in,
+                device_id=at_region((region + n) % nregion),
+                device_id_type=MESH,
+            ).start()
+            return carry
+
+        lax.fori_loop(1, nregion, one, 0)
+        answers[region] = answer[...]
+
     lax.fori_loop(2, nk, spread, 0)
 
     span = WIN * cols
@@ -257,6 +327,31 @@
             device_id={"z": other // nc, "c": other % nc},
             device_id_type=MESH,
         )
+
+    nl, ll = ny, lev // ny
+
+    def hand_columns(start, count):
+        for j in range(start, start + count):
+            for t in range(2):
+                turned = acc[t, j].T.astype(BF)
+                for q in range(nl):
+                    p = (t * nxl + j // half) * ny + q
+                    parts[p, j % half] = turned[q * ll : (q + 1) * ll]
+        for j in range(start, start + count):
+            for t in range(2):
+                for q in range(nl):
+                    p = (t * nxl + j // half) * ny + q
+
+                    @pl.when(p != team)
+                    def _():
+                        pltpu.make_async_remote_copy(
+                            src_ref=parts.at[p, j % half],
+                            dst_ref=sums.at[team, j % half],
+                            send_sem=p_go,
+                            recv_sem=p_in,
+                            device_id=at_team(p),
+                            device_id_type=MESH,
+                        ).start()
 
     sends = (block < blocks - 1, block > 0)
     gets = (block > 0, block < blocks - 1)
@@ -301,8 +396,14 @@
                 for t in range(2):
                     acc[t, j + n] += fine[t, j + n].astype(F32) * part
 
+            @pl.when(k == nk - 1)
+            def _():
+                hand_columns(j, 2)
+
     def wait_all_but_one(k, sem):
         wait_bytes(sent.at[k, pl.ds(0, ndest - 1)], sem.at[k])
+
+    share = members // (nk - 1)
 
     def step(k, carry):
         @pl.when(k < nk)
@@ -324,6 +425,18 @@
             def _():
                 send(k + 2)
 
+            @pl.when(k == 1)
+            def _():
+                gather_system()
+
+            @pl.when(k >= 1)
+            def _():
+                lax.fori_loop((k - 1) * share, k * share, eliminate, 0)
+
+            @pl.when(k == nk - 1)
+            def _():
+                hand_answer()
+
         @pl.when(k >= 1)
         def _():
             localize(k - 1)
@@ -332,30 +445,6 @@
 
     lax.fori_loop(0, nk + 1, step, 0)
 
-    nl, ll = ny, lev // ny
-
-    def flip(j, carry):
-        for t in range(2):
-            turned = acc[t, j].T.astype(BF)
-            for q in range(nl):
-                parts[(t * nxl + j // half) * ny + q, j % half] = turned[q * ll : (q + 1) * ll]
-        return carry
-
-    lax.fori_loop(0, cols, flip, 0)
-
-    def hand_over(n, carry):
-        p = (team + n) % nteam
-        pltpu.make_async_remote_copy(
-            src_ref=parts.at[p],
-            dst_ref=sums.at[team],
-            send_sem=p_go,
-            recv_sem=p_in,
-            device_id=at_team(p),
-            device_id_type=MESH,
-        ).start()
-        return carry
-
-    lax.fori_loop(1, nteam, hand_over, 0)
     sums[team] = parts[team]
     wait_bytes(sums.at[pl.ds(0, nteam - 1)], p_in)
     for j in range(half):
@@ -364,7 +453,6 @@
             value = value + sums[p, j].astype(F32)
         total[j] = value * scale
 
-    from_c, from_block = xl, (z * nc + c)
     dest = (tile * 2) % (blocks * nxl) + xl
     d_block = dest % blocks
     stays = dest == tile
@@ -398,6 +486,11 @@
     lax.fori_loop(0, nk, left, 0)
     wait_bytes(ctrl.at[pl.ds(0, (nteam - 1) * quarter_cols)], f_go)
     wait_bytes(sums.at[pl.ds(0, nteam - 1)], p_go)
+    wait_bytes(grams.at[pl.ds(0, nregion - 1)], g_go)
+    wait_bytes(answers.at[pl.ds(0, nregion - 1)], w_go)
+    wait_bytes(answers.at[pl.ds(0, nregion - 1)], w_in)
+    for g in range(nregion):
+        w_ref[pl.ds(g, 1), :] = answers[g, :1, :]
     for side in range(nxl):
         here = (to_z == z) & (to_c == c) & (xl == side)
 
@@ -410,36 +503,6 @@
         move.wait()
 
     o_ref[...] = moved[...]
-
-
-def solve_weights(gram_sums, right_side):
-    member_count = gram_sums.shape[-1]
-    system = gram_sums + (member_count - 1) * jnp.eye(member_count, dtype=F32)
-    factor = jnp.linalg.cholesky(system)
-    halfway = lax.linalg.triangular_solve(factor, right_side[..., None], left_side=True, lower=True)
-    result = lax.linalg.triangular_solve(
-        factor, halfway, left_side=True, lower=True, transpose_a=True
-    )
-    return result[..., 0]
-
-
-def letkf(hx_pert, innov, obs_prec, obs_region):
-    observed = hx_pert[0]
-    members = observed.shape[0]
-    weighted = (observed * obs_prec[0][None, :]).astype(BF)
-    labels = lax.broadcasted_iota(jnp.int32, (NREG, observed.shape[1]), 0)
-    member_of = obs_region[0][None, :] == labels
-    masked = jnp.where(member_of[:, None, :], weighted[None], jnp.zeros((), BF))
-    gram = jnp.einsum("rko,jo->rkj", masked, observed, preferred_element_type=F32)
-    innov_rows = jnp.where(member_of, innov[0][None, :], 0.0)
-    right = jnp.dot(innov_rows, weighted.astype(F32).T)
-    packed = jnp.concatenate([gram.reshape(NREG, -1), right], axis=1)
-    arrived = lax.all_to_all(packed[:, None], ("xh", "y"), split_axis=0, concat_axis=0, tiled=True)
-    total = jnp.sum(arrived, axis=0)
-    size = members * members
-    own = solve_weights(total[:, :size].reshape(-1, members, members), total[:, size:])
-    everyone = from_everyone(own, ("xh", "y"))
-    return everyone.reshape(NREG, members)
 
 
 def body(
@@ -468,6 +531,7 @@
     total_members = hx_pert.shape[1]
     nteam = nxh * nxl * ny
     quarter = half // ny
+    lanes = 128
 
     x = ens_coarse.reshape(members, lev * own_rows, coarse_cols)
     rwt = jnp.pad(row_weights.T, ((0, 0), (0, 125)))
@@ -479,11 +543,14 @@
 
     vm = pl.BlockSpec(memory_space=pltpu.VMEM)
     dma = pltpu.SemaphoreType.DMA
-    increment = pl.pallas_call(
+    increment, weights = pl.pallas_call(
         lambda *refs: main_kernel((nxh, nxl, nz, nc, ny, 1.0 / (total_members - 1)), refs),
-        in_specs=[vm] * 7,
-        out_specs=vm,
-        out_shape=jax.ShapeDtypeStruct((half, lev // ny, fine_rows), F32),
+        in_specs=[vm] * 11,
+        out_specs=(vm, vm),
+        out_shape=(
+            jax.ShapeDtypeStruct((half, lev // ny, fine_rows), F32),
+            jax.ShapeDtypeStruct((NREG, lanes), F32),
+        ),
         scratch_shapes=[
             pltpu.VMEM((own_rows * lev, own_rows * lev), BF),
             pltpu.VMEM((group, nxh * tiles, own_rows, cols, lev), BF),
@@ -502,6 +569,11 @@
             pltpu.VMEM((nteam, half, lev // ny, fine_rows), BF),
             pltpu.VMEM((half, lev // ny, fine_rows), F32),
             pltpu.VMEM((half, lev // ny, fine_rows), F32),
+            pltpu.VMEM((NREG, total_members, lanes), F32),
+            pltpu.VMEM((NREG, total_members, lanes), F32),
+            pltpu.VMEM((total_members, lanes), F32),
+            pltpu.VMEM((8, lanes), F32),
+            pltpu.VMEM((NREG, 8, lanes), F32),
             dma((group,)),
             dma((group,)),
             dma((group, 2)),
@@ -512,18 +584,14 @@
             dma,
             dma((2,)),
             dma((2,)),
-            dma,
-            dma,
-            dma,
-            dma,
+            *[dma] * 8,
         ],
         compiler_params=pltpu.CompilerParams(
             collective_id=0, has_side_effects=True, vmem_limit_bytes=62 << 20
         ),
-    )(x, col_interp, rwt, mine, band, row_loc, lev_two)
+    )(x, col_interp, rwt, mine, band, row_loc, lev_two, hx_pert[0], innov, obs_prec, obs_region)
     increment = jnp.transpose(increment, (1, 0, 2))
-    weights = letkf(hx_pert, innov, obs_prec, obs_region)
-    return (increment[None], weights)
+    return (increment[None], weights[:, :total_members])
 
 
 def solution(mesh):

time: 269 us -> 222 us (0.83)
  the two profiles are of different devices: /device:TPU:94 before, /device:TPU:3 now
where the time goes in v3:
time: 222 us; the launch traced here: 221 us
  Pallas kernels  212 us (95%)
  local copies, waits for them, and re-layouts  6.3 us (3%)
    pallas_call x1, Pallas kernels, body(): pl.pallas_call(lambda *refs: main_kernel((nxh, nxl, nz, nc, ny, 1.0 / (to...  212 us
    unnamed x7, local copies, waits for them, and re-layouts  5.56 us

profile of v3, /device:TPU:3, one launch (start us, length us, event | category | flops | bytes accessed | tf_op | source)
XLA Modules:
  0.0 221.4 jit_solution(5082417574241153623)
XLA Ops:
  0.6 0.0 copy-start
  0.6 1.4 pad_convert_fusion.refs_4_
  2.0 0.9 copy.15
  2.9 0.8 copy.13
  3.7 0.6 pad.12.refs_2_
  4.3 0.7 fusion.2.refs_6_
  5.0 0.0 copy-done
  5.0 0.1 constant_dynamic-slice_fusion
  5.1 0.8 copy.17
  5.9 212.4 %shard_map.122 = (f32[8,32,256]{2,1,0:T(8,128)}, f32[8,128]{1,0:T(8,128)}) custom-call(bf16[20,512,128]{2,1,0:T(8,128)(2,1)} %bitcast.13, bf16[256,128]{1,0:T(8,128)(2,1)} %refs_1_.1, bf16[256,128]{1,0:T(8,128)(2,1)} %pad.12.refs_2_, bf16[2,256,128]{2,1,0:T(8,128)(2,1)} %bitcast.14, f32[8,128]{1,0:T(8,128)} %pad_convert_fusion.refs_4_, ...), custom_call_target="tpu_custom_call" | custom-call | tf_op jit(solution)/shard_map/pallas_call | solution.py:546
  218.3 1.8 copy.16
  220.1 1.3 copy.19
Async XLA Ops:
  0.6 4.4 %copy-start = (f32[1,128,8,256]{3,2,1,0:T(8,128)S(1)}, f32[1,128,8,256]{3,2,1,0:T(8,128)}, u32[]{:S(2)}) copy-start(f32[1,128,8,256]{3,2,1,0:T(8,128)} %param.14) | copy-start | bytes 3145732

commit v4 on v3

--- a/solution.py
+++ b/solution.py
@@ -29,9 +29,9 @@
 
 def main_kernel(sizes, refs):
     nxh, nxl, nz, nc, ny, scale = sizes
-    x_ref, ci_ref, rwt_ref, cq_ref, band_ref, row_ref, lev_ref, *refs = refs
+    x_ref, ci_ref, rw_ref, cq_ref, band_in, row_ref, lev_in, *refs = refs
     hx_ref, innov_ref, prec_ref, region_ref, o_ref, w_ref, *refs = refs
-    perm, sent, land, sten, stage, ctrl, bands, bandf, field, halo, fine, banded, acc, *refs = refs
+    lev_ref, band_ref, rw_all, perm, sent, land, sten, stage, ctrl, bands, bandf, field, halo, fine, banded, acc, *refs = refs
     parts, sums, total, moved, gram, grams, system, answer, answers, *sems = refs
     s_go, s_in, h_go, h_in, c_go, c_in, f_go, f_in, b_go, b_in, p_go, p_in, m_go, m_in, *sems = sems
     g_go, g_in, w_go, w_in = sems
@@ -117,6 +117,8 @@
     def wait_bytes(ref, sem):
         pltpu.make_async_copy(ref, ref, sem).wait()
 
+    band_ref[...] = jnp.zeros_like(band_ref)
+    band_ref[:, : band_in.shape[1]] = band_in[...].astype(F32)
     spread(0, 0)
     pl.semaphore_wait(barrier, ndest - 1 + nteam - nxh * nxl)
 
@@ -182,6 +184,14 @@
 
     lax.fori_loop(1, nteam, forward, 0)
     ctrl[pl.ds(slot, quarter_cols)] = stage[...]
+
+    def rest(k, carry):
+        spread(k, 0)
+        send(k)
+        return carry
+
+    lax.fori_loop(2, nk, rest, 0)
+
     members, obs = hx_ref.shape
     lanes = gram.shape[2]
     region = xh * ny + y
@@ -255,19 +265,31 @@
         lax.fori_loop(1, nregion, one, 0)
         answers[region] = answer[...]
 
-    lax.fori_loop(2, nk, spread, 0)
-
     span = WIN * cols
     p_id = lax.broadcasted_iota(jnp.int32, (cols * GR, span), 0)
     q_id = lax.broadcasted_iota(jnp.int32, (cols * GR, span), 1)
     same = q_id % cols == p_id // GR
+
+    rw_all[...] = jnp.zeros_like(rw_all)
+    rw_all[:3, :] = rw_ref[...].astype(F32)
+    lev_t = lax.dot_general(
+        one_hot((lev, lev), lambda p: p, lambda q: q),
+        lev_in[...],
+        (((1,), (1,)), ((), ())),
+        preferred_element_type=F32,
+    ).astype(BF)
+    lev_ref[...] = jnp.zeros_like(lev_ref)
+    lev_ref[:lev, :lev] = lev_t
+    lev_ref[lev:, lev:] = lev_t
 
     def stencil(g, carry):
         take = (
             lax.broadcasted_iota(jnp.int32, (cols * GR, groups * GR), 1)
             == lax.broadcasted_iota(jnp.int32, (cols * GR, groups * GR), 0) % GR + g * GR
         ).astype(BF)
-        w = jnp.dot(take, rwt_ref[...], preferred_element_type=F32)
+        w = lax.dot_general(
+            take, rw_all[...].astype(BF), (((1,), (1,)), ((), ())), preferred_element_type=F32
+        )
         start = jnp.minimum(jnp.maximum(g * (GR // 2) - 1, 0), coarse - WIN)
         full = jnp.zeros((cols * GR, span), F32)
         for s in range(3):
@@ -311,6 +333,8 @@
         for group in range(groups):
             rows = pl.ds(group * GR, GR)
             first, second = refine_group(k, group)
+            fine[k % 2, 0, :, rows, :] = first
+            fine[k % 2, 1, :, rows, :] = second
             both = first.astype(F32) * ctrl[pl.ds(0, cols), rows, :].astype(F32)
             both = both + second.astype(F32) * ctrl[pl.ds(cols, cols), rows, :].astype(F32)
             both = both.astype(BF)
@@ -367,10 +391,6 @@
             def _():
                 halo[k, side] = jnp.zeros(halo.shape[2:], BF)
 
-        for group in range(groups):
-            rows = pl.ds(group * GR, GR)
-            for t, part in enumerate(refine_group(k, group)):
-                fine[t, :, rows, :] = part
         for group in range(0, groups, 2):
             sides = []
             for g in (group, group + 1):
@@ -387,14 +407,14 @@
                 banded[:, pl.ds(g * GR, GR), :] = mixed[:, n * lev : (n + 1) * lev].reshape(
                     cols, GR, lev
                 )
-        for j in range(0, cols, 2):
+        for j in [base + jj for jj in range(0, half, 2) for base in (0, half)]:
             pair = jnp.concatenate([banded[j], banded[j + 1]], axis=1)
             mixed = jnp.dot(row_ref[...], pair, preferred_element_type=F32).astype(BF)
             local = jnp.dot(mixed, lev_ref[...], preferred_element_type=F32)
             for n in range(2):
                 part = local[:, n * lev : (n + 1) * lev]
                 for t in range(2):
-                    acc[t, j + n] += fine[t, j + n].astype(F32) * part
+                    acc[t, j + n] += fine[k % 2, t, j + n].astype(F32) * part
 
             @pl.when(k == nk - 1)
             def _():
@@ -421,10 +441,6 @@
                 def _():
                     halo_copy(k, side).start()
 
-            @pl.when(k + 2 < nk)
-            def _():
-                send(k + 2)
-
             @pl.when(k == 1)
             def _():
                 gather_system()
@@ -447,31 +463,29 @@
 
     sums[team] = parts[team]
     wait_bytes(sums.at[pl.ds(0, nteam - 1)], p_in)
+    dest = (tile * 2) % (blocks * nxl) + xl
+    d_block = dest % blocks
+    stays = dest == tile
     for j in range(half):
         value = sums[0, j].astype(F32)
         for p in range(1, nteam):
             value = value + sums[p, j].astype(F32)
-        total[j] = value * scale
-
-    dest = (tile * 2) % (blocks * nxl) + xl
-    d_block = dest % blocks
-    stays = dest == tile
-    move = pltpu.make_async_remote_copy(
-        src_ref=total,
-        dst_ref=moved,
-        send_sem=m_go,
-        recv_sem=m_in,
-        device_id={"xl": dest // blocks, "z": d_block // nc, "c": d_block % nc},
-        device_id_type=MESH,
-    )
-
-    @pl.when(jnp.logical_not(stays))
-    def _():
-        move.start()
-
-    @pl.when(stays)
-    def _():
-        moved[...] = total[...]
+        total[j] = (value * scale).astype(BF)
+
+        @pl.when(jnp.logical_not(stays))
+        def _():
+            pltpu.make_async_remote_copy(
+                src_ref=total.at[j],
+                dst_ref=moved.at[j],
+                send_sem=m_go,
+                recv_sem=m_in,
+                device_id={"xl": dest // blocks, "z": d_block // nc, "c": d_block % nc},
+                device_id_type=MESH,
+            ).start()
+
+        @pl.when(stays)
+        def _():
+            moved[j] = total[j]
 
     def left(k, carry):
         wait_all_but_one(k, s_go)
@@ -490,7 +504,7 @@
     wait_bytes(answers.at[pl.ds(0, nregion - 1)], w_go)
     wait_bytes(answers.at[pl.ds(0, nregion - 1)], w_in)
     for g in range(nregion):
-        w_ref[pl.ds(g, 1), :] = answers[g, :1, :]
+        w_ref[pl.ds(g, 1), :] = answers[g, :1, :members]
     for side in range(nxl):
         here = (to_z == z) & (to_c == c) & (xl == side)
 
@@ -500,9 +514,11 @@
 
     @pl.when(jnp.logical_not(stays))
     def _():
-        move.wait()
-
-    o_ref[...] = moved[...]
+        wait_bytes(total, m_go)
+        wait_bytes(moved, m_in)
+
+    for j in range(half):
+        o_ref[:, j, :] = moved[j].astype(F32)
 
 
 def body(
@@ -534,12 +550,8 @@
     lanes = 128
 
     x = ens_coarse.reshape(members, lev * own_rows, coarse_cols)
-    rwt = jnp.pad(row_weights.T, ((0, 0), (0, 125)))
     mine = lax.dynamic_slice_in_dim(ctrl_vec[0], lax.axis_index("y") * quarter, quarter, 1)
     mine = jnp.transpose(mine.astype(BF), (1, 2, 0))
-    band = jnp.pad(band_loc.astype(F32), ((0, 0), (0, 128 - band_loc.shape[1])))
-    none = jnp.zeros_like(level_loc)
-    lev_two = jnp.block([[level_loc.T, none], [none, level_loc.T]])
 
     vm = pl.BlockSpec(memory_space=pltpu.VMEM)
     dma = pltpu.SemaphoreType.DMA
@@ -548,27 +560,30 @@
         in_specs=[vm] * 11,
         out_specs=(vm, vm),
         out_shape=(
-            jax.ShapeDtypeStruct((half, lev // ny, fine_rows), F32),
-            jax.ShapeDtypeStruct((NREG, lanes), F32),
+            jax.ShapeDtypeStruct((lev // ny, half, fine_rows), F32),
+            jax.ShapeDtypeStruct((NREG, total_members), F32),
         ),
         scratch_shapes=[
+            pltpu.VMEM((2 * lev, 2 * lev), BF),
+            pltpu.VMEM((half, lanes), F32),
+            pltpu.VMEM((8, fine_rows), F32),
             pltpu.VMEM((own_rows * lev, own_rows * lev), BF),
             pltpu.VMEM((group, nxh * tiles, own_rows, cols, lev), BF),
             pltpu.VMEM((group, nxh, coarse, cols, lev), BF),
             pltpu.VMEM((fine_rows // GR, cols * GR, WIN * cols), BF),
             pltpu.VMEM((quarter, fine_rows, lev), BF),
             pltpu.VMEM((nxh * cols, fine_rows, lev), BF),
-            pltpu.VMEM((2, *band.shape), F32),
+            pltpu.VMEM((2, half, lanes), F32),
             pltpu.VMEM((cols * GR, 4 * half * GR), BF),
             pltpu.VMEM((group, 2, half, fine_rows, lev), BF),
             pltpu.VMEM((group, 2, half, fine_rows, lev), BF),
-            pltpu.VMEM((nxh, cols, fine_rows, lev), BF),
+            pltpu.VMEM((2, nxh, cols, fine_rows, lev), BF),
             pltpu.VMEM((cols, fine_rows, lev), BF),
             pltpu.VMEM((nxh, cols, fine_rows, lev), F32),
             pltpu.VMEM((nteam, half, lev // ny, fine_rows), BF),
             pltpu.VMEM((nteam, half, lev // ny, fine_rows), BF),
-            pltpu.VMEM((half, lev // ny, fine_rows), F32),
-            pltpu.VMEM((half, lev // ny, fine_rows), F32),
+            pltpu.VMEM((half, lev // ny, fine_rows), BF),
+            pltpu.VMEM((half, lev // ny, fine_rows), BF),
             pltpu.VMEM((NREG, total_members, lanes), F32),
             pltpu.VMEM((NREG, total_members, lanes), F32),
             pltpu.VMEM((total_members, lanes), F32),
@@ -589,9 +604,8 @@
         compiler_params=pltpu.CompilerParams(
             collective_id=0, has_side_effects=True, vmem_limit_bytes=62 << 20
         ),
-    )(x, col_interp, rwt, mine, band, row_loc, lev_two, hx_pert[0], innov, obs_prec, obs_region)
-    increment = jnp.transpose(increment, (1, 0, 2))
-    return (increment[None], weights[:, :total_members])
+    )(x, col_interp, row_weights, mine, band_loc, row_loc, level_loc, hx_pert[0], innov, obs_prec, obs_region)
+    return (increment[None], weights)
 
 
 def solution(mesh):

time: 222 us -> 208 us (0.937)
  the two profiles are of different devices: /device:TPU:3 before, /device:TPU:2 now
where the time goes in v4:
time: 208 us; the launch traced here: 207 us
  Pallas kernels  202 us (97%)
  local copies, waits for them, and re-layouts  5.05 us (2%)
    pallas_call x1, Pallas kernels, body(): pl.pallas_call(lambda *refs: main_kernel((nxh, nxl, nz, nc, ny, 1.0 / (to...  202 us
    unnamed x5, local copies, waits for them, and re-layouts  4.94 us

profile of v4, /device:TPU:2, one launch (start us, length us, event | category | flops | bytes accessed | tf_op | source)
XLA Modules:
  0.0 207.4 jit_solution(5179845219135557992)
XLA Ops:
  0.6 0.0 copy-start
  0.6 1.2 copy-done
  1.9 0.1 constant_dynamic-slice_fusion
  2.0 0.8 copy.14
  2.8 201.7 %shard_map.122 = (f32[32,8,256]{2,1,0:T(8,128)}, f32[8,80]{1,0:T(8,128)}) custom-call(bf16[20,512,128]{2,1,0:T(8,128)(2,1)} %bitcast.8, bf16[256,128]{1,0:T(8,128)(2,1)} %refs_1_.1, bf16[3,256]{1,0:T(4,128)(2,1)} %refs_2_.1, bf16[2,256,128]{2,1,0:T(8,128)(2,1)} %bitcast.9, bf16[8,24]{1,0:T(8,128)(2,1)} %refs_4_.1, bf16[256,256]{1,0:T(8,128)(2,1)} %refs_5_.1, ...), custom_call_target="tpu_custom_call" | custom-call | tf_op jit(solution)/shard_map/pallas_call | solution.py:558
  204.4 1.7 copy.17
  206.1 1.3 copy.18
Async XLA Ops:
  0.6 1.2 copy-start

commit v5 on v4

--- a/solution.py
+++ b/solution.py
@@ -185,12 +185,9 @@
     lax.fori_loop(1, nteam, forward, 0)
     ctrl[pl.ds(slot, quarter_cols)] = stage[...]
 
-    def rest(k, carry):
-        spread(k, 0)
-        send(k)
-        return carry
-
-    lax.fori_loop(2, nk, rest, 0)
+    spread(2, 0)
+    send(2)
+    lax.fori_loop(3, nk, spread, 0)
 
     members, obs = hx_ref.shape
     lanes = gram.shape[2]
@@ -333,8 +330,8 @@
         for group in range(groups):
             rows = pl.ds(group * GR, GR)
             first, second = refine_group(k, group)
-            fine[k % 2, 0, :, rows, :] = first
-            fine[k % 2, 1, :, rows, :] = second
+            fine[k % 3, 0, :, rows, :] = first
+            fine[k % 3, 1, :, rows, :] = second
             both = first.astype(F32) * ctrl[pl.ds(0, cols), rows, :].astype(F32)
             both = both + second.astype(F32) * ctrl[pl.ds(cols, cols), rows, :].astype(F32)
             both = both.astype(BF)
@@ -414,7 +411,7 @@
             for n in range(2):
                 part = local[:, n * lev : (n + 1) * lev]
                 for t in range(2):
-                    acc[t, j + n] += fine[k % 2, t, j + n].astype(F32) * part
+                    acc[t, j + n] += fine[k % 3, t, j + n].astype(F32) * part
 
             @pl.when(k == nk - 1)
             def _():
@@ -423,7 +420,7 @@
     def wait_all_but_one(k, sem):
         wait_bytes(sent.at[k, pl.ds(0, ndest - 1)], sem.at[k])
 
-    share = members // (nk - 1)
+    share = -(-members // (nk - 2))
 
     def step(k, carry):
         @pl.when(k < nk)
@@ -441,25 +438,30 @@
                 def _():
                     halo_copy(k, side).start()
 
+            @pl.when(k + 3 < nk)
+            def _():
+                send(k + 3)
+
             @pl.when(k == 1)
             def _():
                 gather_system()
 
             @pl.when(k >= 1)
             def _():
-                lax.fori_loop((k - 1) * share, k * share, eliminate, 0)
+                last = jnp.minimum(k * share, members)
+                lax.fori_loop(jnp.minimum((k - 1) * share, members), last, eliminate, 0)
 
             @pl.when(k == nk - 1)
             def _():
                 hand_answer()
 
-        @pl.when(k >= 1)
-        def _():
-            localize(k - 1)
-
-        return carry
-
-    lax.fori_loop(0, nk + 1, step, 0)
+        @pl.when(k >= 2)
+        def _():
+            localize(k - 2)
+
+        return carry
+
+    lax.fori_loop(0, nk + 2, step, 0)
 
     sums[team] = parts[team]
     wait_bytes(sums.at[pl.ds(0, nteam - 1)], p_in)
@@ -518,7 +520,7 @@
         wait_bytes(moved, m_in)
 
     for j in range(half):
-        o_ref[:, j, :] = moved[j].astype(F32)
+        o_ref[j] = moved[j]
 
 
 def body(
@@ -560,7 +562,7 @@
         in_specs=[vm] * 11,
         out_specs=(vm, vm),
         out_shape=(
-            jax.ShapeDtypeStruct((lev // ny, half, fine_rows), F32),
+            jax.ShapeDtypeStruct((half, lev // ny, fine_rows), BF),
             jax.ShapeDtypeStruct((NREG, total_members), F32),
         ),
         scratch_shapes=[
@@ -577,7 +579,7 @@
             pltpu.VMEM((cols * GR, 4 * half * GR), BF),
             pltpu.VMEM((group, 2, half, fine_rows, lev), BF),
             pltpu.VMEM((group, 2, half, fine_rows, lev), BF),
-            pltpu.VMEM((2, nxh, cols, fine_rows, lev), BF),
+            pltpu.VMEM((3, nxh, cols, fine_rows, lev), BF),
             pltpu.VMEM((cols, fine_rows, lev), BF),
             pltpu.VMEM((nxh, cols, fine_rows, lev), F32),
             pltpu.VMEM((nteam, half, lev // ny, fine_rows), BF),
@@ -605,6 +607,7 @@
             collective_id=0, has_side_effects=True, vmem_limit_bytes=62 << 20
         ),
     )(x, col_interp, row_weights, mine, band_loc, row_loc, level_loc, hx_pert[0], innov, obs_prec, obs_region)
+    increment = jnp.transpose(increment, (1, 0, 2)).astype(F32)
     return (increment[None], weights)
 
 

time: 208 us -> 203 us (0.976)
  Pallas kernels: 202 us -> 196 us
    pallas_call x1, Pallas kernels: 202 us -> 196 us  [body(): pl.pallas_call(lambda *refs: main_kernel((nxh, nxl, nz, nc, ny, 1.0 / (to...]
where the time goes in v5:
time: 203 us; the launch traced here: 202 us
  Pallas kernels  196 us (97%)
  local copies, waits for them, and re-layouts  4.23 us (2%)
    pallas_call x1, Pallas kernels, body(): pl.pallas_call(lambda *refs: main_kernel((nxh, nxl, nz, nc, ny, 1.0 / (to...  196 us
    unnamed x5, local copies, waits for them, and re-layouts  4.12 us

profile of v5, /device:TPU:2, one launch (start us, length us, event | category | flops | bytes accessed | tf_op | source)
XLA Modules:
  0.0 202.0 jit_solution(1928285601761747880)
XLA Ops:
  0.6 0.0 copy-start
  0.6 1.2 copy-done
  1.9 0.1 constant_dynamic-slice_fusion
  2.0 0.8 copy.15
  2.8 196.2 %shard_map.122 = (bf16[8,32,256]{2,1,0:T(8,128)(2,1)}, f32[8,80]{1,0:T(8,128)}) custom-call(bf16[20,512,128]{2,1,0:T(8,128)(2,1)} %bitcast.11, bf16[256,128]{1,0:T(8,128)(2,1)} %refs_1_.1, bf16[3,256]{1,0:T(4,128)(2,1)} %refs_2_.1, bf16[2,256,128]{2,1,0:T(8,128)(2,1)} %bitcast.12, bf16[8,24]{1,0:T(8,128)(2,1)} %refs_4_.1, bf16[256,256]{1,0:T(8,128)(2,1)} %refs_5_.1, ...), custom_call_target="tpu_custom_call" | custom-call | tf_op jit(solution)/shard_map/pallas_call | solution.py:560
  199.0 0.9 convert_bitcast_fusion
  199.9 0.9 copy.14
  200.7 1.3 copy.17
Async XLA Ops:
  0.6 1.2 copy-start

commit v6 on v4

--- a/solution.py
+++ b/solution.py
@@ -31,7 +31,7 @@
     nxh, nxl, nz, nc, ny, scale = sizes
     x_ref, ci_ref, rw_ref, cq_ref, band_in, row_ref, lev_in, *refs = refs
     hx_ref, innov_ref, prec_ref, region_ref, o_ref, w_ref, *refs = refs
-    lev_ref, band_ref, rw_all, perm, sent, land, sten, stage, ctrl, bands, bandf, field, halo, fine, banded, acc, *refs = refs
+    lev_ref, band_ref, rw_all, perm, sent, land, sten, stage, ctrl, bands, bandf, field, fine, banded, acc, *refs = refs
     parts, sums, total, moved, gram, grams, system, answer, answers, *sems = refs
     s_go, s_in, h_go, h_in, c_go, c_in, f_go, f_in, b_go, b_in, p_go, p_in, m_go, m_in, *sems = sems
     g_go, g_in, w_go, w_in = sems
@@ -317,7 +317,10 @@
     full = jnp.dot(take_col, wide, preferred_element_type=F32)
     p_id2 = lax.broadcasted_iota(jnp.int32, full.shape, 0)
     q_id2 = lax.broadcasted_iota(jnp.int32, full.shape, 1)
-    bandf[...] = jnp.where(p_id2 % GR == q_id2 % GR, full, 0.0).astype(BF)
+    full = jnp.where(p_id2 % GR == q_id2 % GR, full, 0.0).astype(BF)
+    side_rows = half * GR
+    for i in range(2):
+        bandf[i] = full[i * side_rows : (i + 1) * side_rows, i * side_rows : (i + 3) * side_rows]
 
     acc[...] = jnp.zeros_like(acc)
 
@@ -333,19 +336,19 @@
         for group in range(groups):
             rows = pl.ds(group * GR, GR)
             first, second = refine_group(k, group)
-            fine[k % 2, 0, :, rows, :] = first
-            fine[k % 2, 1, :, rows, :] = second
+            fine[k, 0, :, rows, :] = first
+            fine[k, 1, :, rows, :] = second
             both = first.astype(F32) * ctrl[pl.ds(0, cols), rows, :].astype(F32)
             both = both + second.astype(F32) * ctrl[pl.ds(cols, cols), rows, :].astype(F32)
             both = both.astype(BF)
-            field[k, 0, :, rows, :] = both[:half]
-            field[k, 1, :, rows, :] = both[half:]
+            field[k, 1, :, rows, :] = both[:half]
+            field[k, 2, :, rows, :] = both[half:]
 
     def halo_copy(k, side):
         other = block + 1 if side == 0 else block - 1
         return pltpu.make_async_remote_copy(
-            src_ref=field.at[k, 1 - side],
-            dst_ref=halo.at[k, side],
+            src_ref=field.at[k, 2 - side],
+            dst_ref=field.at[k, 3 * side],
             send_sem=h_go.at[k, side],
             recv_sem=h_in.at[k, side],
             device_id={"z": other // nc, "c": other % nc},
@@ -354,23 +357,22 @@
 
     nl, ll = ny, lev // ny
 
-    def hand_columns(start, count):
+    def hand_columns(i, start, count):
         for j in range(start, start + count):
             for t in range(2):
-                turned = acc[t, j].T.astype(BF)
+                turned = acc[t, i * half + j].T.astype(BF)
                 for q in range(nl):
-                    p = (t * nxl + j // half) * ny + q
-                    parts[p, j % half] = turned[q * ll : (q + 1) * ll]
+                    parts[(t * nxl + i) * ny + q, j] = turned[q * ll : (q + 1) * ll]
         for j in range(start, start + count):
             for t in range(2):
                 for q in range(nl):
-                    p = (t * nxl + j // half) * ny + q
+                    p = (t * nxl + i) * ny + q
 
                     @pl.when(p != team)
                     def _():
                         pltpu.make_async_remote_copy(
-                            src_ref=parts.at[p, j % half],
-                            dst_ref=sums.at[team, j % half],
+                            src_ref=parts.at[p, j],
+                            dst_ref=sums.at[team, j],
                             send_sem=p_go,
                             recv_sem=p_in,
                             device_id=at_team(p),
@@ -378,52 +380,49 @@
                         ).start()
 
     sends = (block < blocks - 1, block > 0)
-    gets = (block > 0, block < blocks - 1)
-
-    def localize(k):
-        for side in range(2):
-
-            @pl.when(gets[side])
-            def _():
-                wait_bytes(halo.at[k, side], h_in.at[k, side])
-
-            @pl.when(jnp.logical_not(gets[side]))
-            def _():
-                halo[k, side] = jnp.zeros(halo.shape[2:], BF)
+    near = 1 - c
+    edge = ((c == 0) & (block == 0)) | ((c == nc - 1) & (block == blocks - 1))
+
+    def localize(k, i, side):
+        @pl.when((side == near) | jnp.logical_not(edge))
+        def _():
+            wait_bytes(field.at[k, 3 * side], h_in.at[k, side])
+
+        @pl.when((side != near) & edge)
+        def _():
+            field[k, 3 * side] = jnp.zeros(field.shape[2:], BF)
 
         for group in range(0, groups, 2):
-            sides = []
+            wide = []
             for g in (group, group + 1):
                 rows = pl.ds(g * GR, GR)
-                pieces = [
-                    ref[:, rows, :].reshape(half * GR, lev)
-                    for ref in (halo.at[k, 0], field.at[k, 0], field.at[k, 1], halo.at[k, 1])
-                ]
-                sides.append(jnp.concatenate(pieces, axis=0))
+                pieces = [field[k, i + n, :, rows, :].reshape(half * GR, lev) for n in range(3)]
+                wide.append(jnp.concatenate(pieces, axis=0))
             mixed = jnp.dot(
-                bandf[...], jnp.concatenate(sides, axis=1), preferred_element_type=F32
+                bandf[i], jnp.concatenate(wide, axis=1), preferred_element_type=F32
             ).astype(BF)
             for n, g in enumerate((group, group + 1)):
                 banded[:, pl.ds(g * GR, GR), :] = mixed[:, n * lev : (n + 1) * lev].reshape(
-                    cols, GR, lev
+                    half, GR, lev
                 )
-        for j in [base + jj for jj in range(0, half, 2) for base in (0, half)]:
+        for j in range(0, half, 2):
             pair = jnp.concatenate([banded[j], banded[j + 1]], axis=1)
             mixed = jnp.dot(row_ref[...], pair, preferred_element_type=F32).astype(BF)
             local = jnp.dot(mixed, lev_ref[...], preferred_element_type=F32)
             for n in range(2):
                 part = local[:, n * lev : (n + 1) * lev]
+                at = i * half + j + n
                 for t in range(2):
-                    acc[t, j + n] += fine[k % 2, t, j + n].astype(F32) * part
+                    acc[t, at] += fine[k, t, at].astype(F32) * part
 
             @pl.when(k == nk - 1)
             def _():
-                hand_columns(j, 2)
+                hand_columns(i, j, 2)
 
     def wait_all_but_one(k, sem):
         wait_bytes(sent.at[k, pl.ds(0, ndest - 1)], sem.at[k])
 
-    share = members // (nk - 1)
+    share = -(-members // (nk - 2))
 
     def step(k, carry):
         @pl.when(k < nk)
@@ -447,19 +446,26 @@
 
             @pl.when(k >= 1)
             def _():
-                lax.fori_loop((k - 1) * share, k * share, eliminate, 0)
+                last = jnp.minimum(k * share, members)
+                lax.fori_loop(jnp.minimum((k - 1) * share, members), last, eliminate, 0)
 
             @pl.when(k == nk - 1)
             def _():
                 hand_answer()
 
+        first = (k >= 1) & (k <= nk)
+
         @pl.when(k >= 1)
         def _():
-            localize(k - 1)
-
-        return carry
-
-    lax.fori_loop(0, nk + 1, step, 0)
+            localize(
+                jnp.where(first, k - 1, k - 1 - nk),
+                jnp.where(first, near, 1 - near),
+                jnp.where(first, near, 1 - near),
+            )
+
+        return carry
+
+    lax.fori_loop(0, 2 * nk + 1, step, 0)
 
     sums[team] = parts[team]
     wait_bytes(sums.at[pl.ds(0, nteam - 1)], p_in)
@@ -518,7 +524,7 @@
         wait_bytes(moved, m_in)
 
     for j in range(half):
-        o_ref[:, j, :] = moved[j].astype(F32)
+        o_ref[j] = moved[j]
 
 
 def body(
@@ -560,7 +566,7 @@
         in_specs=[vm] * 11,
         out_specs=(vm, vm),
         out_shape=(
-            jax.ShapeDtypeStruct((lev // ny, half, fine_rows), F32),
+            jax.ShapeDtypeStruct((half, lev // ny, fine_rows), BF),
             jax.ShapeDtypeStruct((NREG, total_members), F32),
         ),
         scratch_shapes=[
@@ -574,11 +580,10 @@
             pltpu.VMEM((quarter, fine_rows, lev), BF),
             pltpu.VMEM((nxh * cols, fine_rows, lev), BF),
             pltpu.VMEM((2, half, lanes), F32),
-            pltpu.VMEM((cols * GR, 4 * half * GR), BF),
-            pltpu.VMEM((group, 2, half, fine_rows, lev), BF),
-            pltpu.VMEM((group, 2, half, fine_rows, lev), BF),
-            pltpu.VMEM((2, nxh, cols, fine_rows, lev), BF),
-            pltpu.VMEM((cols, fine_rows, lev), BF),
+            pltpu.VMEM((2, half * GR, 3 * half * GR), BF),
+            pltpu.VMEM((group, 4, half, fine_rows, lev), BF),
+            pltpu.VMEM((group, nxh, cols, fine_rows, lev), BF),
+            pltpu.VMEM((half, fine_rows, lev), BF),
             pltpu.VMEM((nxh, cols, fine_rows, lev), F32),
             pltpu.VMEM((nteam, half, lev // ny, fine_rows), BF),
             pltpu.VMEM((nteam, half, lev // ny, fine_rows), BF),
@@ -605,6 +610,7 @@
             collective_id=0, has_side_effects=True, vmem_limit_bytes=62 << 20
         ),
     )(x, col_interp, row_weights, mine, band_loc, row_loc, level_loc, hx_pert[0], innov, obs_prec, obs_region)
+    increment = jnp.transpose(increment, (1, 0, 2)).astype(F32)
     return (increment[None], weights)
 
 

time: 208 us -> 192 us (0.923)
  Pallas kernels: 202 us -> 186 us
    pallas_call x1, Pallas kernels: 202 us -> 186 us  [body(): pl.pallas_call(lambda *refs: main_kernel((nxh, nxl, nz, nc, ny, 1.0 / (to...]
where the time goes in v6:
time: 192 us
  Pallas kernels  186 us (97%)
  local copies, waits for them, and re-layouts  4.23 us (2%)
    pallas_call x1, Pallas kernels, body(): pl.pallas_call(lambda *refs: main_kernel((nxh, nxl, nz, nc, ny, 1.0 / (to...  186 us
    unnamed x5, local copies, waits for them, and re-layouts  4.12 us

profile of v6, /device:TPU:2, one launch (start us, length us, event | category | flops | bytes accessed | tf_op | source)
XLA Modules:
  0.0 191.9 jit_solution(16757809394195393696)
XLA Ops:
  0.6 0.0 copy-start
  0.6 1.2 copy-done
  1.9 0.1 constant_dynamic-slice_fusion
  2.0 0.8 copy.15
  2.8 186.1 %shard_map.122 = (bf16[8,32,256]{2,1,0:T(8,128)(2,1)}, f32[8,80]{1,0:T(8,128)}) custom-call(bf16[20,512,128]{2,1,0:T(8,128)(2,1)} %bitcast.11, bf16[256,128]{1,0:T(8,128)(2,1)} %refs_1_.1, bf16[3,256]{1,0:T(4,128)(2,1)} %refs_2_.1, bf16[2,256,128]{2,1,0:T(8,128)(2,1)} %bitcast.12, bf16[8,24]{1,0:T(8,128)(2,1)} %refs_4_.1, bf16[256,256]{1,0:T(8,128)(2,1)} %refs_5_.1, ...), custom_call_target="tpu_custom_call" | custom-call | tf_op jit(solution)/shard_map/pallas_call | solution.py:564
  188.8 0.9 convert_bitcast_fusion
  189.8 0.9 copy.14
  190.6 1.3 copy.17
Async XLA Ops:
  0.6 1.2 copy-start

commit v7 on v6

--- a/solution.py
+++ b/solution.py
@@ -32,7 +32,7 @@
     x_ref, ci_ref, rw_ref, cq_ref, band_in, row_ref, lev_in, *refs = refs
     hx_ref, innov_ref, prec_ref, region_ref, o_ref, w_ref, *refs = refs
     lev_ref, band_ref, rw_all, perm, sent, land, sten, stage, ctrl, bands, bandf, field, fine, banded, acc, *refs = refs
-    parts, sums, total, moved, gram, grams, system, answer, answers, *sems = refs
+    parts, sums, total, moved, turned_out, gram, grams, system, answer, answers, *sems = refs
     s_go, s_in, h_go, h_in, c_go, c_in, f_go, f_in, b_go, b_in, p_go, p_in, m_go, m_in, *sems = sems
     g_go, g_in, w_go, w_in = sems
 
@@ -374,7 +374,7 @@
                             src_ref=parts.at[p, j],
                             dst_ref=sums.at[team, j],
                             send_sem=p_go,
-                            recv_sem=p_in,
+                            recv_sem=p_in.at[j],
                             device_id=at_team(p),
                             device_id_type=MESH,
                         ).start()
@@ -422,6 +422,34 @@
     def wait_all_but_one(k, sem):
         wait_bytes(sent.at[k, pl.ds(0, ndest - 1)], sem.at[k])
 
+    dest = (tile * 2) % (blocks * nxl) + xl
+    d_block = dest % blocks
+    stays = dest == tile
+
+    def finish():
+        for j in range(half):
+            wait_bytes(sums.at[pl.ds(0, nteam - 1), j], p_in.at[j])
+            sums[team, j] = parts[team, j]
+            value = sums[0, j].astype(F32)
+            for p in range(1, nteam):
+                value = value + sums[p, j].astype(F32)
+            total[j] = (value * scale).astype(BF)
+
+            @pl.when(jnp.logical_not(stays))
+            def _():
+                pltpu.make_async_remote_copy(
+                    src_ref=total.at[j],
+                    dst_ref=moved.at[j],
+                    send_sem=m_go,
+                    recv_sem=m_in,
+                    device_id={"xl": dest // blocks, "z": d_block // nc, "c": d_block % nc},
+                    device_id_type=MESH,
+                ).start()
+
+            @pl.when(stays)
+            def _():
+                moved[j] = total[j]
+
     share = -(-members // (nk - 2))
 
     def step(k, carry):
@@ -452,6 +480,10 @@
             @pl.when(k == nk - 1)
             def _():
                 hand_answer()
+
+        @pl.when((k == 2 * nk) & (xl == near))
+        def _():
+            finish()
 
         first = (k >= 1) & (k <= nk)
 
@@ -467,31 +499,9 @@
 
     lax.fori_loop(0, 2 * nk + 1, step, 0)
 
-    sums[team] = parts[team]
-    wait_bytes(sums.at[pl.ds(0, nteam - 1)], p_in)
-    dest = (tile * 2) % (blocks * nxl) + xl
-    d_block = dest % blocks
-    stays = dest == tile
-    for j in range(half):
-        value = sums[0, j].astype(F32)
-        for p in range(1, nteam):
-            value = value + sums[p, j].astype(F32)
-        total[j] = (value * scale).astype(BF)
-
-        @pl.when(jnp.logical_not(stays))
-        def _():
-            pltpu.make_async_remote_copy(
-                src_ref=total.at[j],
-                dst_ref=moved.at[j],
-                send_sem=m_go,
-                recv_sem=m_in,
-                device_id={"xl": dest // blocks, "z": d_block // nc, "c": d_block % nc},
-                device_id_type=MESH,
-            ).start()
-
-        @pl.when(stays)
-        def _():
-            moved[j] = total[j]
+    @pl.when(xl != near)
+    def _():
+        finish()
 
     def left(k, carry):
         wait_all_but_one(k, s_go)
@@ -524,7 +534,8 @@
         wait_bytes(moved, m_in)
 
     for j in range(half):
-        o_ref[j] = moved[j]
+        turned_out[:, j, :] = moved[j].astype(F32)
+    o_ref[...] = turned_out[...].astype(BF)
 
 
 def body(
@@ -566,7 +577,7 @@
         in_specs=[vm] * 11,
         out_specs=(vm, vm),
         out_shape=(
-            jax.ShapeDtypeStruct((half, lev // ny, fine_rows), BF),
+            jax.ShapeDtypeStruct((lev // ny, half, fine_rows), BF),
             jax.ShapeDtypeStruct((NREG, total_members), F32),
         ),
         scratch_shapes=[
@@ -589,6 +600,7 @@
             pltpu.VMEM((nteam, half, lev // ny, fine_rows), BF),
             pltpu.VMEM((half, lev // ny, fine_rows), BF),
             pltpu.VMEM((half, lev // ny, fine_rows), BF),
+            pltpu.VMEM((lev // ny, half, fine_rows), F32),
             pltpu.VMEM((NREG, total_members, lanes), F32),
             pltpu.VMEM((NREG, total_members, lanes), F32),
             pltpu.VMEM((total_members, lanes), F32),
@@ -598,20 +610,18 @@
             dma((group,)),
             dma((group, 2)),
             dma((group, 2)),
-            dma,
-            dma,
-            dma,
-            dma,
+            *[dma] * 4,
             dma((2,)),
             dma((2,)),
-            *[dma] * 8,
+            dma,
+            dma((half,)),
+            *[dma] * 6,
         ],
         compiler_params=pltpu.CompilerParams(
             collective_id=0, has_side_effects=True, vmem_limit_bytes=62 << 20
         ),
     )(x, col_interp, row_weights, mine, band_loc, row_loc, level_loc, hx_pert[0], innov, obs_prec, obs_region)
-    increment = jnp.transpose(increment, (1, 0, 2)).astype(F32)
-    return (increment[None], weights)
+    return (increment.astype(F32)[None], weights)
 
 
 def solution(mesh):

time: 192 us -> 193 us (level)
  Pallas kernels: 186 us -> 188 us
    unnamed x5 -> x4, local copies, waits for them, and re-layouts: 4.12 us -> 3.26 us
where the time goes in v7:
time: 193 us
  Pallas kernels  188 us (97%)
  local copies, waits for them, and re-layouts  3.37 us (2%)
    pallas_call x1, Pallas kernels, body(): pl.pallas_call(lambda *refs: main_kernel((nxh, nxl, nz, nc, ny, 1.0 / (to...  188 us

profile of v7, /device:TPU:2, one launch (start us, length us, event | category | flops | bytes accessed | tf_op | source)
XLA Modules:
  0.0 193.2 jit_solution(9101901860521494775)
XLA Ops:
  0.6 0.0 copy-start
  0.6 1.2 copy-done
  1.9 0.1 constant_dynamic-slice_fusion
  2.0 0.8 copy.14
  2.8 187.6 %shard_map.122 = (bf16[32,8,256]{2,1,0:T(8,128)(2,1)}, f32[8,80]{1,0:T(8,128)}) custom-call(bf16[20,512,128]{2,1,0:T(8,128)(2,1)} %bitcast.10, bf16[256,128]{1,0:T(8,128)(2,1)} %refs_1_.1, bf16[3,256]{1,0:T(4,128)(2,1)} %refs_2_.1, bf16[2,256,128]{2,1,0:T(8,128)(2,1)} %bitcast.11, bf16[8,24]{1,0:T(8,128)(2,1)} %refs_4_.1, bf16[256,256]{1,0:T(8,128)(2,1)} %refs_5_.1, ...), custom_call_target="tpu_custom_call" | custom-call | tf_op jit(solution)/shard_map/pallas_call | solution.py:575
  190.3 1.6 bitcast_convert_fusion
  192.0 1.3 copy.16
Async XLA Ops:
  0.6 1.2 copy-start

commit v8 on v7

--- a/solution.py
+++ b/solution.py
@@ -42,14 +42,19 @@
     half = cols // 2
     blocks = nz * nc
     xh, xl, z, c, y = (lax.axis_index(a) for a in ("xh", "xl", "z", "c", "y"))
-    block = z * nc + c
-    tile = xl * blocks + block
+    shift = nz // 2
+    block = (z + nz - shift) % nz * nc + c
+    tile = xl * blocks + z * nc + c
+
+    def z_of(b):
+        return (b // nc + shift) % nz
+
     me = (xh * nxl + xl) * blocks + block
     team = (xh * nxl + xl) * ny + y
 
     def at_dest(d):
         m, b = d // blocks, d % blocks
-        return {"xh": m // nxl, "xl": m % nxl, "z": b // nc, "c": b % nc}
+        return {"xh": m // nxl, "xl": m % nxl, "z": z_of(b), "c": b % nc}
 
     def at_team(p):
         m = p // ny
@@ -122,7 +127,7 @@
     spread(0, 0)
     pl.semaphore_wait(barrier, ndest - 1 + nteam - nxh * nxl)
 
-    to_xl, to_z, to_c = c, (xl * nz + z) // nc, (xl * nz + z) % nc
+    to_xl, to_z, to_c = c, z_of(xl * nz + z), (xl * nz + z) % nc
     home = (to_xl == xl) & (to_z == z) & (to_c == c)
     quarter = pltpu.make_async_remote_copy(
         src_ref=cq_ref,
@@ -351,7 +356,7 @@
             dst_ref=field.at[k, 3 * side],
             send_sem=h_go.at[k, side],
             recv_sem=h_in.at[k, side],
-            device_id={"z": other // nc, "c": other % nc},
+            device_id={"z": z_of(other), "c": other % nc},
             device_id_type=MESH,
         )
 
@@ -422,7 +427,7 @@
     def wait_all_but_one(k, sem):
         wait_bytes(sent.at[k, pl.ds(0, ndest - 1)], sem.at[k])
 
-    dest = (tile * 2) % (blocks * nxl) + xl
+    dest = block * nxl + xl
     d_block = dest % blocks
     stays = dest == tile
 
@@ -481,10 +486,6 @@
             def _():
                 hand_answer()
 
-        @pl.when((k == 2 * nk) & (xl == near))
-        def _():
-            finish()
-
         first = (k >= 1) & (k <= nk)
 
         @pl.when(k >= 1)
@@ -499,9 +500,7 @@
 
     lax.fori_loop(0, 2 * nk + 1, step, 0)
 
-    @pl.when(xl != near)
-    def _():
-        finish()
+    finish()
 
     def left(k, carry):
         wait_all_but_one(k, s_go)

time: 193 us -> 187 us (0.969)
  the two profiles are of different devices: /device:TPU:2 before, /device:TPU:64 now
where the time goes in v8:
time: 187 us
  Pallas kernels  181 us (97%)
  local copies, waits for them, and re-layouts  3.37 us (2%)
    pallas_call x1, Pallas kernels, body(): pl.pallas_call(lambda *refs: main_kernel((nxh, nxl, nz, nc, ny, 1.0 / (to...  181 us

profile of v8, /device:TPU:64, one launch (start us, length us, event | category | flops | bytes accessed | tf_op | source)
XLA Modules:
  0.0 186.8 jit_solution(5037287790189091209)
XLA Ops:
  0.6 0.0 copy-start
  0.6 1.2 copy-done
  1.9 0.1 constant_dynamic-slice_fusion
  2.0 0.8 copy.14
  2.8 181.2 %shard_map.122 = (bf16[32,8,256]{2,1,0:T(8,128)(2,1)}, f32[8,80]{1,0:T(8,128)}) custom-call(bf16[20,512,128]{2,1,0:T(8,128)(2,1)} %bitcast.10, bf16[256,128]{1,0:T(8,128)(2,1)} %refs_1_.1, bf16[3,256]{1,0:T(4,128)(2,1)} %refs_2_.1, bf16[2,256,128]{2,1,0:T(8,128)(2,1)} %bitcast.11, bf16[8,24]{1,0:T(8,128)(2,1)} %refs_4_.1, bf16[256,256]{1,0:T(8,128)(2,1)} %refs_5_.1, ...), custom_call_target="tpu_custom_call" | custom-call | tf_op jit(solution)/shard_map/pallas_call | solution.py:574
  183.9 1.6 bitcast_convert_fusion
  185.6 1.3 copy.16
Async XLA Ops:
  0.6 1.2 copy-start

commit v9 on v8

--- a/solution.py
+++ b/solution.py
@@ -29,9 +29,9 @@
 
 def main_kernel(sizes, refs):
     nxh, nxl, nz, nc, ny, scale = sizes
-    x_ref, ci_ref, rw_ref, cq_ref, band_in, row_ref, lev_in, *refs = refs
+    x_ref, ci_ref, rw_ref, cv_ref, band_in, row_ref, lev_in, *refs = refs
     hx_ref, innov_ref, prec_ref, region_ref, o_ref, w_ref, *refs = refs
-    lev_ref, band_ref, rw_all, perm, sent, land, sten, stage, ctrl, bands, bandf, field, fine, banded, acc, *refs = refs
+    cq_ref, lev_ref, band_ref, rw_all, perm, sent, land, sten, stage, ctrl, bands, bandf, field, fine, banded, acc, *refs = refs
     parts, sums, total, moved, turned_out, gram, grams, system, answer, answers, *sems = refs
     s_go, s_in, h_go, h_in, c_go, c_in, f_go, f_in, b_go, b_in, p_go, p_in, m_go, m_in, *sems = sems
     g_go, g_in, w_go, w_in = sems
@@ -122,6 +122,8 @@
     def wait_bytes(ref, sem):
         pltpu.make_async_copy(ref, ref, sem).wait()
 
+    for n in range(cq_ref.shape[0]):
+        cq_ref[n] = cv_ref[:, y * cq_ref.shape[0] + n, :].T.astype(BF)
     band_ref[...] = jnp.zeros_like(band_ref)
     band_ref[:, : band_in.shape[1]] = band_in[...].astype(F32)
     spread(0, 0)
@@ -457,8 +459,10 @@
 
     share = -(-members // (nk - 2))
 
-    def step(k, carry):
-        @pl.when(k < nk)
+    def step(n, carry):
+        k = jnp.minimum(n, nk - 1)
+
+        @pl.when((n <= nk - 2) | (n == nk + 2))
         def _():
             wait_all_but_one(k, s_in)
 
@@ -473,28 +477,30 @@
                 def _():
                     halo_copy(k, side).start()
 
-            @pl.when(k == 1)
-            def _():
-                gather_system()
-
-            @pl.when(k >= 1)
-            def _():
-                last = jnp.minimum(k * share, members)
-                lax.fori_loop(jnp.minimum((k - 1) * share, members), last, eliminate, 0)
-
-            @pl.when(k == nk - 1)
-            def _():
-                hand_answer()
-
-        first = (k >= 1) & (k <= nk)
-
-        @pl.when(k >= 1)
-        def _():
-            localize(
-                jnp.where(first, k - 1, k - 1 - nk),
-                jnp.where(first, near, 1 - near),
-                jnp.where(first, near, 1 - near),
-            )
+        @pl.when(n == 1)
+        def _():
+            gather_system()
+
+        @pl.when((n >= 1) & (n <= nk - 2))
+        def _():
+            last = jnp.minimum(n * share, members)
+            lax.fori_loop(jnp.minimum((n - 1) * share, members), last, eliminate, 0)
+
+        @pl.when(n == nk - 1)
+        def _():
+            hand_answer()
+
+        inner = (n <= nk - 1) | (n == nk + 2)
+        member = jnp.where(
+            inner,
+            jnp.where(n <= nk - 1, n - 1, nk - 1),
+            jnp.where(n <= nk + 1, n - nk, n - nk - 1),
+        )
+        which = jnp.where(inner, near, 1 - near)
+
+        @pl.when(n >= 1)
+        def _():
+            localize(member, which, which)
 
         return carry
 
@@ -566,8 +572,6 @@
     lanes = 128
 
     x = ens_coarse.reshape(members, lev * own_rows, coarse_cols)
-    mine = lax.dynamic_slice_in_dim(ctrl_vec[0], lax.axis_index("y") * quarter, quarter, 1)
-    mine = jnp.transpose(mine.astype(BF), (1, 2, 0))
 
     vm = pl.BlockSpec(memory_space=pltpu.VMEM)
     dma = pltpu.SemaphoreType.DMA
@@ -580,6 +584,7 @@
             jax.ShapeDtypeStruct((NREG, total_members), F32),
         ),
         scratch_shapes=[
+            pltpu.VMEM((quarter, fine_rows, lev), BF),
             pltpu.VMEM((2 * lev, 2 * lev), BF),
             pltpu.VMEM((half, lanes), F32),
             pltpu.VMEM((8, fine_rows), F32),
@@ -619,7 +624,7 @@
         compiler_params=pltpu.CompilerParams(
             collective_id=0, has_side_effects=True, vmem_limit_bytes=62 << 20
         ),
-    )(x, col_interp, row_weights, mine, band_loc, row_loc, level_loc, hx_pert[0], innov, obs_prec, obs_region)
+    )(x, col_interp, row_weights, ctrl_vec[0], band_loc, row_loc, level_loc, hx_pert[0], innov, obs_prec, obs_region)
     return (increment.astype(F32)[None], weights)
 
 

time: 187 us -> 188 us (level)
  Pallas kernels: 181 us -> 184 us
  local copies, waits for them, and re-layouts: 3.37 us -> 1.28 us
    pallas_call x1, Pallas kernels: 181 us -> 184 us  [body(): pl.pallas_call(lambda *refs: main_kernel((nxh, nxl, nz, nc, ny, 1.0 / (to...]
    unnamed x4 -> x1, local copies, waits for them, and re-layouts: 3.26 us -> 1.28 us
where the time goes in v9:
time: 188 us
  Pallas kernels  184 us (98%)
    pallas_call x1, Pallas kernels, body(): pl.pallas_call(lambda *refs: main_kernel((nxh, nxl, nz, nc, ny, 1.0 / (to...  184 us

profile of v9, /device:TPU:64, one launch (start us, length us, event | category | flops | bytes accessed | tf_op | source)
XLA Modules:
  0.0 187.6 jit_solution(3231530142548352664)
XLA Ops:
  0.6 184.0 %shard_map.122 = (bf16[32,8,256]{2,1,0:T(8,128)(2,1)}, f32[8,80]{1,0:T(8,128)}) custom-call(bf16[20,512,128]{2,1,0:T(8,128)(2,1)} %bitcast.6, bf16[256,128]{1,0:T(8,128)(2,1)} %refs_1_.1, bf16[3,256]{1,0:T(4,128)(2,1)} %refs_2_.1, f32[128,8,256]{2,1,0:T(8,128)} %bitcast.7, bf16[8,24]{1,0:T(8,128)(2,1)} %refs_4_.1, bf16[256,256]{1,0:T(8,128)(2,1)} %refs_5_.1, ...), custom_call_target="tpu_custom_call" | custom-call | tf_op jit(solution)/shard_map/pallas_call | solution.py:578
  184.7 1.6 bitcast_convert_fusion
  186.3 1.3 copy.14

commit v10 on v8

--- a/solution.py
+++ b/solution.py
@@ -29,9 +29,9 @@
 
 def main_kernel(sizes, refs):
     nxh, nxl, nz, nc, ny, scale = sizes
-    x_ref, ci_ref, rw_ref, cq_ref, band_in, row_ref, lev_in, *refs = refs
+    x_ref, ci_ref, rw_ref, cv_ref, band_in, row_ref, lev_in, *refs = refs
     hx_ref, innov_ref, prec_ref, region_ref, o_ref, w_ref, *refs = refs
-    lev_ref, band_ref, rw_all, perm, sent, land, sten, stage, ctrl, bands, bandf, field, fine, banded, acc, *refs = refs
+    cq_ref, lev_ref, band_ref, rw_all, perm, sent, land, sten, stage, ctrl, bands, bandf, field, fine, banded, acc, *refs = refs
     parts, sums, total, moved, turned_out, gram, grams, system, answer, answers, *sems = refs
     s_go, s_in, h_go, h_in, c_go, c_in, f_go, f_in, b_go, b_in, p_go, p_in, m_go, m_in, *sems = sems
     g_go, g_in, w_go, w_in = sems
@@ -122,6 +122,8 @@
     def wait_bytes(ref, sem):
         pltpu.make_async_copy(ref, ref, sem).wait()
 
+    for n in range(cq_ref.shape[0]):
+        cq_ref[n] = cv_ref[:, y * cq_ref.shape[0] + n, :].T.astype(BF)
     band_ref[...] = jnp.zeros_like(band_ref)
     band_ref[:, : band_in.shape[1]] = band_in[...].astype(F32)
     spread(0, 0)
@@ -566,8 +568,6 @@
     lanes = 128
 
     x = ens_coarse.reshape(members, lev * own_rows, coarse_cols)
-    mine = lax.dynamic_slice_in_dim(ctrl_vec[0], lax.axis_index("y") * quarter, quarter, 1)
-    mine = jnp.transpose(mine.astype(BF), (1, 2, 0))
 
     vm = pl.BlockSpec(memory_space=pltpu.VMEM)
     dma = pltpu.SemaphoreType.DMA
@@ -580,6 +580,7 @@
             jax.ShapeDtypeStruct((NREG, total_members), F32),
         ),
         scratch_shapes=[
+            pltpu.VMEM((quarter, fine_rows, lev), BF),
             pltpu.VMEM((2 * lev, 2 * lev), BF),
             pltpu.VMEM((half, lanes), F32),
             pltpu.VMEM((8, fine_rows), F32),
@@ -619,7 +620,7 @@
         compiler_params=pltpu.CompilerParams(
             collective_id=0, has_side_effects=True, vmem_limit_bytes=62 << 20
         ),
-    )(x, col_interp, row_weights, mine, band_loc, row_loc, level_loc, hx_pert[0], innov, obs_prec, obs_region)
+    )(x, col_interp, row_weights, ctrl_vec[0], band_loc, row_loc, level_loc, hx_pert[0], innov, obs_prec, obs_region)
     return (increment.astype(F32)[None], weights)
 
 

time: 187 us -> 185 us (0.989)
  local copies, waits for them, and re-layouts: 3.37 us -> 1.28 us
    unnamed x4 -> x1, local copies, waits for them, and re-layouts: 3.26 us -> 1.28 us
where the time goes in v10:
time: 185 us
  Pallas kernels  182 us (98%)
    pallas_call x1, Pallas kernels, body(): pl.pallas_call(lambda *refs: main_kernel((nxh, nxl, nz, nc, ny, 1.0 / (to...  182 us

profile of v10, /device:TPU:64, one launch (start us, length us, event | category | flops | bytes accessed | tf_op | source)
XLA Modules:
  0.0 185.3 jit_solution(711581266930514908)
XLA Ops:
  0.6 181.8 %shard_map.122 = (bf16[32,8,256]{2,1,0:T(8,128)(2,1)}, f32[8,80]{1,0:T(8,128)}) custom-call(bf16[20,512,128]{2,1,0:T(8,128)(2,1)} %bitcast.6, bf16[256,128]{1,0:T(8,128)(2,1)} %refs_1_.1, bf16[3,256]{1,0:T(4,128)(2,1)} %refs_2_.1, f32[128,8,256]{2,1,0:T(8,128)} %bitcast.7, bf16[8,24]{1,0:T(8,128)(2,1)} %refs_4_.1, bf16[256,256]{1,0:T(8,128)(2,1)} %refs_5_.1, ...), custom_call_target="tpu_custom_call" | custom-call | tf_op jit(solution)/shard_map/pallas_call | solution.py:574
  182.4 1.6 bitcast_convert_fusion
  184.0 1.3 copy.14
